TPU v7x, 32 devices: a 4x2x2 block of a 4x4x8 slice. The times are simulated.
32 devices in a mesh: dp: 4 (over y, z), tp: 8 (over x, core).
Axes of the slice: x: 4, y: 2, z: 2, core: 2. Of those that a mesh axis runs over, the one named last changes fastest.
The devices are a block of a 4x4x8 slice.
Arguments:
- token_ids: int32 [128, 128], P('dp'), parts along dimension 0
- emb_table: bfloat16 [16384, 1024], P('tp')
- gain_vec: bfloat16 [1024], replicated
- w_qkv: bfloat16 [1024, 11264], P(None, 'tp')
- grad_u: bfloat16 [128, 128, 11264], P('dp', None, 'tp'), parts along dimension 0
- grad_res: bfloat16 [128, 128, 1024], P('dp', 'tp'), parts along dimension 0
Outputs:
- output 1: bfloat16 [128, 128, 11264], P('dp', None, 'tp'), parts along dimension 0
- output 2: bfloat16 [128, 128, 1024], P('dp', 'tp'), parts along dimension 0
- output 3: float32 [65536, 1024], P(('dp', 'tp')), parts along dimension 0
- output 4: float32 [1024, 45056], P(None, ('dp', 'tp')), parts along dimension 1
- output 5: float32 [4096], P('dp'), parts along dimension 0
There are 4 independent parts. A program takes and returns all parts, laid end to end along the dimension named above; an argument that names none is the same for every part.
All inputs are finite; a program needn't handle non-finite values.
Results may differ from a plain program's by a relative error of at most 0.00497064.
Values are sent between devices in bfloat16 or wider.
A program may use at most 768 MiB of HBM per device.

v0:
```python
import jax
import jax.numpy as jnp
from jax import lax
from jax.sharding import PartitionSpec as P, NamedSharding

NORM_EPS = 1e-6


def solution(mesh):
    group_size = mesh.shape['tp']

    def local_step(token_ids, table_loc, gain_vec, w_loc, du_loc, dres_loc):
        seq_len = token_ids.shape[1]
        rows_loc, model_dim = table_loc.shape
        seq_loc = seq_len // group_size
        cols_loc = w_loc.shape[1]
        dev_idx = lax.axis_index('tp')
        row_start = dev_idx * rows_loc
        tok_start = dev_idx * seq_loc
        gain_f = gain_vec.astype(jnp.float32)

        def micro_step(acc_state, inputs):
            grad_table, grad_w, grad_gain = acc_state
            tok_ids, du_m, dres_m = inputs
            local_ids = tok_ids - row_start
            in_block = (local_ids >= 0) & (local_ids < rows_loc)
            safe_ids = jnp.where(in_block, local_ids, 0)
            looked = jnp.take(table_loc, safe_ids, axis=0)
            partial_x = jnp.where(in_block[:, None], looked, jnp.zeros_like(looked))
            tokens = lax.psum(partial_x, 'tp')
            tok_f = tokens.astype(jnp.float32)
            inv_rms = lax.rsqrt(jnp.mean(tok_f * tok_f, axis=-1, keepdims=True) + NORM_EPS)
            n_hat = tok_f * inv_rms
            normed = (n_hat * gain_f).astype(jnp.bfloat16)
            u_m = jnp.dot(normed, w_loc, preferred_element_type=jnp.float32).astype(jnp.bfloat16)
            x_own = lax.dynamic_slice_in_dim(tokens, tok_start, seq_loc, axis=0)
            dn_part = lax.dot_general(du_m, w_loc, (((1,), (1,)), ((), ())), preferred_element_type=jnp.float32).astype(jnp.bfloat16)
            dn_recv = lax.all_to_all(dn_part.reshape(group_size, seq_loc, model_dim), 'tp', 0, 0, tiled=True)
            d_norm = jnp.sum(dn_recv, axis=0, dtype=jnp.float32)
            hat_own = lax.dynamic_slice_in_dim(n_hat, tok_start, seq_loc, axis=0)
            inv_own = lax.dynamic_slice_in_dim(inv_rms, tok_start, seq_loc, axis=0)
            gain_dn = gain_f * d_norm
            centre = jnp.mean(hat_own * gain_dn, axis=-1, keepdims=True)
            d_x = (dres_m.astype(jnp.float32) + inv_own * (gain_dn - hat_own * centre)).astype(jnp.bfloat16)
            grad_gain = grad_gain + jnp.sum(d_norm * hat_own, axis=0)
            grad_w = grad_w + lax.dot_general(normed, du_m, (((0,), (0,)), ((), ())), preferred_element_type=jnp.float32)
            dx_all = lax.all_gather(d_x, 'tp', axis=0, tiled=True)
            contrib = jnp.where(in_block[:, None], dx_all.astype(jnp.float32), 0.0)
            grad_table = grad_table + jax.ops.segment_sum(contrib, safe_ids, num_segments=rows_loc)
            return (grad_table, grad_w, grad_gain), (u_m, x_own)

        init_state = (jnp.zeros((rows_loc, model_dim), jnp.float32), jnp.zeros((model_dim, cols_loc), jnp.float32), jnp.zeros((model_dim,), jnp.float32))
        (grad_table, grad_w, grad_gain), (u_proj, x_resid) = lax.scan(micro_step, init_state, (token_ids, du_loc, dres_loc))
        grad_gain = lax.psum(grad_gain, 'tp')
        return u_proj, x_resid, grad_table, grad_w, grad_gain

    return jax.shard_map(local_step, mesh=mesh,
                         in_specs=(P('dp', None), P('tp', None), P(None), P(None, 'tp'), P('dp', None, 'tp'), P('dp', 'tp', None)),
                         out_specs=(P('dp', None, 'tp'), P('dp', 'tp', None), P(('dp', 'tp'), None), P(None, ('dp', 'tp')), P('dp')),
                         check_vma=False)
```

profile of v0, /device:TPU:81, one launch (start us, length us, event | category | flops | bytes accessed | tf_op | source)
XLA Modules:
  0.0 3082.5 jit_solution(4910501593746995925)
XLA Ops:
  12.5 3050.9 %while.21 = (s32[]{:T(128)}, f32[2048,1024]{1,0:T(8,128)}, f32[1024,1408]{1,0:T(8,128)}, f32[1024]{0:T(1024)S(1)}, bf16[32,128,1408]{2,1,0:T(8,128)(2,1)}, /*ind...) while((s32[]{:T(128)}, f32[2048,1024]{1,0:T(8,128)}, ...), condition=%wide.region_7.8_spmd.clone, body=%wide.region_0.7_spmd.clone.sunk | while | flops 1113428736 | bytes 34387704 | solution.py:53
  26.6 48.2 %all-reduce.2.cloned.1.call-done = bf16[128,1024]{1,0:T(8,128)(2,1)} async-done(((bf16[128,1024]{1,0:T(8,128)(2,1)}), bf16[128,1024]{1,0:T(8,128)(2,1)}) %all-reduce.2.cloned.1.call-update) | async-done | bytes 262160 | tf_op jit(solution)/shard_map/while/body/eval_jaxpr/psum | solution.py:30
  87.3 15.8 all_gather.7
  123.2 45.1 %all-reduce.2.cloned.1.call-done = bf16[128,1024]{1,0:T(8,128)(2,1)} async-done(((bf16[128,1024]{1,0:T(8,128)(2,1)}), bf16[128,1024]{1,0:T(8,128)(2,1)}) %all-reduce.2.cloned.1.call-update) | async-done | bytes 262160 | tf_op jit(solution)/shard_map/while/body/eval_jaxpr/psum | solution.py:30
  182.5 15.8 all_gather.7
  218.4 45.1 %all-reduce.2.cloned.1.call-done = bf16[128,1024]{1,0:T(8,128)(2,1)} async-done(((bf16[128,1024]{1,0:T(8,128)(2,1)}), bf16[128,1024]{1,0:T(8,128)(2,1)}) %all-reduce.2.cloned.1.call-update) | async-done | bytes 262160 | tf_op jit(solution)/shard_map/while/body/eval_jaxpr/psum | solution.py:30
  277.7 15.8 all_gather.7
  313.6 45.1 %all-reduce.2.cloned.1.call-done = bf16[128,1024]{1,0:T(8,128)(2,1)} async-done(((bf16[128,1024]{1,0:T(8,128)(2,1)}), bf16[128,1024]{1,0:T(8,128)(2,1)}) %all-reduce.2.cloned.1.call-update) | async-done | bytes 262160 | tf_op jit(solution)/shard_map/while/body/eval_jaxpr/psum | solution.py:30
  373.0 15.8 all_gather.7
  408.9 45.1 %all-reduce.2.cloned.1.call-done = bf16[128,1024]{1,0:T(8,128)(2,1)} async-done(((bf16[128,1024]{1,0:T(8,128)(2,1)}), bf16[128,1024]{1,0:T(8,128)(2,1)}) %all-reduce.2.cloned.1.call-update) | async-done | bytes 262160 | tf_op jit(solution)/shard_map/while/body/eval_jaxpr/psum | solution.py:30
  468.2 15.8 all_gather.7
  504.1 45.1 %all-reduce.2.cloned.1.call-done = bf16[128,1024]{1,0:T(8,128)(2,1)} async-done(((bf16[128,1024]{1,0:T(8,128)(2,1)}), bf16[128,1024]{1,0:T(8,128)(2,1)}) %all-reduce.2.cloned.1.call-update) | async-done | bytes 262160 | tf_op jit(solution)/shard_map/while/body/eval_jaxpr/psum | solution.py:30
  563.4 15.8 all_gather.7
  599.3 45.1 %all-reduce.2.cloned.1.call-done = bf16[128,1024]{1,0:T(8,128)(2,1)} async-done(((bf16[128,1024]{1,0:T(8,128)(2,1)}), bf16[128,1024]{1,0:T(8,128)(2,1)}) %all-reduce.2.cloned.1.call-update) | async-done | bytes 262160 | tf_op jit(solution)/shard_map/while/body/eval_jaxpr/psum | solution.py:30
  658.6 15.8 all_gather.7
  694.5 45.1 %all-reduce.2.cloned.1.call-done = bf16[128,1024]{1,0:T(8,128)(2,1)} async-done(((bf16[128,1024]{1,0:T(8,128)(2,1)}), bf16[128,1024]{1,0:T(8,128)(2,1)}) %all-reduce.2.cloned.1.call-update) | async-done | bytes 262160 | tf_op jit(solution)/shard_map/while/body/eval_jaxpr/psum | solution.py:30
  753.9 15.8 all_gather.7
  789.8 45.1 %all-reduce.2.cloned.1.call-done = bf16[128,1024]{1,0:T(8,128)(2,1)} async-done(((bf16[128,1024]{1,0:T(8,128)(2,1)}), bf16[128,1024]{1,0:T(8,128)(2,1)}) %all-reduce.2.cloned.1.call-update) | async-done | bytes 262160 | tf_op jit(solution)/shard_map/while/body/eval_jaxpr/psum | solution.py:30
  849.1 15.8 all_gather.7
  885.0 45.1 %all-reduce.2.cloned.1.call-done = bf16[128,1024]{1,0:T(8,128)(2,1)} async-done(((bf16[128,1024]{1,0:T(8,128)(2,1)}), bf16[128,1024]{1,0:T(8,128)(2,1)}) %all-reduce.2.cloned.1.call-update) | async-done | bytes 262160 | tf_op jit(solution)/shard_map/while/body/eval_jaxpr/psum | solution.py:30
  944.3 15.8 all_gather.7
  980.2 45.1 %all-reduce.2.cloned.1.call-done = bf16[128,1024]{1,0:T(8,128)(2,1)} async-done(((bf16[128,1024]{1,0:T(8,128)(2,1)}), bf16[128,1024]{1,0:T(8,128)(2,1)}) %all-reduce.2.cloned.1.call-update) | async-done | bytes 262160 | tf_op jit(solution)/shard_map/while/body/eval_jaxpr/psum | solution.py:30
  1075.4 45.1 %all-reduce.2.cloned.1.call-done = bf16[128,1024]{1,0:T(8,128)(2,1)} async-done(((bf16[128,1024]{1,0:T(8,128)(2,1)}), bf16[128,1024]{1,0:T(8,128)(2,1)}) %all-reduce.2.cloned.1.call-update) | async-done | bytes 262160 | tf_op jit(solution)/shard_map/while/body/eval_jaxpr/psum | solution.py:30
  1170.6 45.1 %all-reduce.2.cloned.1.call-done = bf16[128,1024]{1,0:T(8,128)(2,1)} async-done(((bf16[128,1024]{1,0:T(8,128)(2,1)}), bf16[128,1024]{1,0:T(8,128)(2,1)}) %all-reduce.2.cloned.1.call-update) | async-done | bytes 262160 | tf_op jit(solution)/shard_map/while/body/eval_jaxpr/psum | solution.py:30
  1230.0 15.8 all_gather.7
  1265.9 45.1 %all-reduce.2.cloned.1.call-done = bf16[128,1024]{1,0:T(8,128)(2,1)} async-done(((bf16[128,1024]{1,0:T(8,128)(2,1)}), bf16[128,1024]{1,0:T(8,128)(2,1)}) %all-reduce.2.cloned.1.call-update) | async-done | bytes 262160 | tf_op jit(solution)/shard_map/while/body/eval_jaxpr/psum | solution.py:30
  1325.2 15.8 all_gather.7
  1361.1 45.1 %all-reduce.2.cloned.1.call-done = bf16[128,1024]{1,0:T(8,128)(2,1)} async-done(((bf16[128,1024]{1,0:T(8,128)(2,1)}), bf16[128,1024]{1,0:T(8,128)(2,1)}) %all-reduce.2.cloned.1.call-update) | async-done | bytes 262160 | tf_op jit(solution)/shard_map/while/body/eval_jaxpr/psum | solution.py:30
  1456.3 45.1 %all-reduce.2.cloned.1.call-done = bf16[128,1024]{1,0:T(8,128)(2,1)} async-done(((bf16[128,1024]{1,0:T(8,128)(2,1)}), bf16[128,1024]{1,0:T(8,128)(2,1)}) %all-reduce.2.cloned.1.call-update) | async-done | bytes 262160 | tf_op jit(solution)/shard_map/while/body/eval_jaxpr/psum | solution.py:30
  1515.6 15.8 all_gather.7
  1551.5 45.1 %all-reduce.2.cloned.1.call-done = bf16[128,1024]{1,0:T(8,128)(2,1)} async-done(((bf16[128,1024]{1,0:T(8,128)(2,1)}), bf16[128,1024]{1,0:T(8,128)(2,1)}) %all-reduce.2.cloned.1.call-update) | async-done | bytes 262160 | tf_op jit(solution)/shard_map/while/body/eval_jaxpr/psum | solution.py:30
  1610.8 15.8 all_gather.7
  1646.7 45.1 %all-reduce.2.cloned.1.call-done = bf16[128,1024]{1,0:T(8,128)(2,1)} async-done(((bf16[128,1024]{1,0:T(8,128)(2,1)}), bf16[128,1024]{1,0:T(8,128)(2,1)}) %all-reduce.2.cloned.1.call-update) | async-done | bytes 262160 | tf_op jit(solution)/shard_map/while/body/eval_jaxpr/psum | solution.py:30
  1742.0 45.1 %all-reduce.2.cloned.1.call-done = bf16[128,1024]{1,0:T(8,128)(2,1)} async-done(((bf16[128,1024]{1,0:T(8,128)(2,1)}), bf16[128,1024]{1,0:T(8,128)(2,1)}) %all-reduce.2.cloned.1.call-update) | async-done | bytes 262160 | tf_op jit(solution)/shard_map/while/body/eval_jaxpr/psum | solution.py:30
  1837.2 45.1 %all-reduce.2.cloned.1.call-done = bf16[128,1024]{1,0:T(8,128)(2,1)} async-done(((bf16[128,1024]{1,0:T(8,128)(2,1)}), bf16[128,1024]{1,0:T(8,128)(2,1)}) %all-reduce.2.cloned.1.call-update) | async-done | bytes 262160 | tf_op jit(solution)/shard_map/while/body/eval_jaxpr/psum | solution.py:30
  1932.4 45.1 %all-reduce.2.cloned.1.call-done = bf16[128,1024]{1,0:T(8,128)(2,1)} async-done(((bf16[128,1024]{1,0:T(8,128)(2,1)}), bf16[128,1024]{1,0:T(8,128)(2,1)}) %all-reduce.2.cloned.1.call-update) | async-done | bytes 262160 | tf_op jit(solution)/shard_map/while/body/eval_jaxpr/psum | solution.py:30
  2027.6 45.1 %all-reduce.2.cloned.1.call-done = bf16[128,1024]{1,0:T(8,128)(2,1)} async-done(((bf16[128,1024]{1,0:T(8,128)(2,1)}), bf16[128,1024]{1,0:T(8,128)(2,1)}) %all-reduce.2.cloned.1.call-update) | async-done | bytes 262160 | tf_op jit(solution)/shard_map/while/body/eval_jaxpr/psum | solution.py:30
  2122.9 45.1 %all-reduce.2.cloned.1.call-done = bf16[128,1024]{1,0:T(8,128)(2,1)} async-done(((bf16[128,1024]{1,0:T(8,128)(2,1)}), bf16[128,1024]{1,0:T(8,128)(2,1)}) %all-reduce.2.cloned.1.call-update) | async-done | bytes 262160 | tf_op jit(solution)/shard_map/while/body/eval_jaxpr/psum | solution.py:30
  2218.1 45.1 %all-reduce.2.cloned.1.call-done = bf16[128,1024]{1,0:T(8,128)(2,1)} async-done(((bf16[128,1024]{1,0:T(8,128)(2,1)}), bf16[128,1024]{1,0:T(8,128)(2,1)}) %all-reduce.2.cloned.1.call-update) | async-done | bytes 262160 | tf_op jit(solution)/shard_map/while/body/eval_jaxpr/psum | solution.py:30
  2313.3 45.1 %all-reduce.2.cloned.1.call-done = bf16[128,1024]{1,0:T(8,128)(2,1)} async-done(((bf16[128,1024]{1,0:T(8,128)(2,1)}), bf16[128,1024]{1,0:T(8,128)(2,1)}) %all-reduce.2.cloned.1.call-update) | async-done | bytes 262160 | tf_op jit(solution)/shard_map/while/body/eval_jaxpr/psum | solution.py:30
  2408.5 45.1 %all-reduce.2.cloned.1.call-done = bf16[128,1024]{1,0:T(8,128)(2,1)} async-done(((bf16[128,1024]{1,0:T(8,128)(2,1)}), bf16[128,1024]{1,0:T(8,128)(2,1)}) %all-reduce.2.cloned.1.call-update) | async-done | bytes 262160 | tf_op jit(solution)/shard_map/while/body/eval_jaxpr/psum | solution.py:30
  2503.8 45.1 %all-reduce.2.cloned.1.call-done = bf16[128,1024]{1,0:T(8,128)(2,1)} async-done(((bf16[128,1024]{1,0:T(8,128)(2,1)}), bf16[128,1024]{1,0:T(8,128)(2,1)}) %all-reduce.2.cloned.1.call-update) | async-done | bytes 262160 | tf_op jit(solution)/shard_map/while/body/eval_jaxpr/psum | solution.py:30
  2599.0 45.1 %all-reduce.2.cloned.1.call-done = bf16[128,1024]{1,0:T(8,128)(2,1)} async-done(((bf16[128,1024]{1,0:T(8,128)(2,1)}), bf16[128,1024]{1,0:T(8,128)(2,1)}) %all-reduce.2.cloned.1.call-update) | async-done | bytes 262160 | tf_op jit(solution)/shard_map/while/body/eval_jaxpr/psum | solution.py:30
  2694.2 45.1 %all-reduce.2.cloned.1.call-done = bf16[128,1024]{1,0:T(8,128)(2,1)} async-done(((bf16[128,1024]{1,0:T(8,128)(2,1)}), bf16[128,1024]{1,0:T(8,128)(2,1)}) %all-reduce.2.cloned.1.call-update) | async-done | bytes 262160 | tf_op jit(solution)/shard_map/while/body/eval_jaxpr/psum | solution.py:30
  2789.4 45.1 %all-reduce.2.cloned.1.call-done = bf16[128,1024]{1,0:T(8,128)(2,1)} async-done(((bf16[128,1024]{1,0:T(8,128)(2,1)}), bf16[128,1024]{1,0:T(8,128)(2,1)}) %all-reduce.2.cloned.1.call-update) | async-done | bytes 262160 | tf_op jit(solution)/shard_map/while/body/eval_jaxpr/psum | solution.py:30
  2884.6 45.1 %all-reduce.2.cloned.1.call-done = bf16[128,1024]{1,0:T(8,128)(2,1)} async-done(((bf16[128,1024]{1,0:T(8,128)(2,1)}), bf16[128,1024]{1,0:T(8,128)(2,1)}) %all-reduce.2.cloned.1.call-update) | async-done | bytes 262160 | tf_op jit(solution)/shard_map/while/body/eval_jaxpr/psum | solution.py:30
  2979.9 45.1 %all-reduce.2.cloned.1.call-done = bf16[128,1024]{1,0:T(8,128)(2,1)} async-done(((bf16[128,1024]{1,0:T(8,128)(2,1)}), bf16[128,1024]{1,0:T(8,128)(2,1)}) %all-reduce.2.cloned.1.call-update) | async-done | bytes 262160 | tf_op jit(solution)/shard_map/while/body/eval_jaxpr/psum | solution.py:30
  3039.2 15.8 all_gather.7
  (858 shorter events, 1382.6 us)
Async XLA Ops:
  12.5 62.4 %all-reduce.2.cloned.1.call-start = ((), (), s32[]{:S(2)}) async-start(), calls=%async_computation.1 | async-start | bytes 524288 | tf_op jit(solution)/shard_map/while/body/eval_jaxpr/psum | solution.py:30
  20.6 64.7 %all-to-all-start = ((bf16[8,16,1024]{2,1,0:T(8,128)(2,1)}), bf16[8,16,1024]{2,1,0:T(8,128)(2,1)S(1)}, u32[]{:S(2)}, u32[]{:S(2)}) async-start(bf16[8,16,1024]{2,1,0:T(8,128)(2,1)} %bitcast.57), calls=%async_computation | async-start | bytes 524288 | tf_op jit(solution)/shard_map/while/body/eval_jaxpr/all_to_all | solution.py:38
  111.6 56.8 %all-reduce.2.cloned.1.call-start = ((), (), s32[]{:S(2)}) async-start(), calls=%async_computation.1 | async-start | bytes 524288 | tf_op jit(solution)/shard_map/while/body/eval_jaxpr/psum | solution.py:30
  119.7 60.9 %all-to-all-start = ((bf16[8,16,1024]{2,1,0:T(8,128)(2,1)}), bf16[8,16,1024]{2,1,0:T(8,128)(2,1)S(1)}, u32[]{:S(2)}, u32[]{:S(2)}) async-start(bf16[8,16,1024]{2,1,0:T(8,128)(2,1)} %bitcast.57), calls=%async_computation | async-start | bytes 524288 | tf_op jit(solution)/shard_map/while/body/eval_jaxpr/all_to_all | solution.py:38
  214.9 60.9 %all-to-all-start = ((bf16[8,16,1024]{2,1,0:T(8,128)(2,1)}), bf16[8,16,1024]{2,1,0:T(8,128)(2,1)S(1)}, u32[]{:S(2)}, u32[]{:S(2)}) async-start(bf16[8,16,1024]{2,1,0:T(8,128)(2,1)} %bitcast.57), calls=%async_computation | async-start | bytes 524288 | tf_op jit(solution)/shard_map/while/body/eval_jaxpr/all_to_all | solution.py:38
  302.0 56.8 %all-reduce.2.cloned.1.call-start = ((), (), s32[]{:S(2)}) async-start(), calls=%async_computation.1 | async-start | bytes 524288 | tf_op jit(solution)/shard_map/while/body/eval_jaxpr/psum | solution.py:30
  310.1 60.9 %all-to-all-start = ((bf16[8,16,1024]{2,1,0:T(8,128)(2,1)}), bf16[8,16,1024]{2,1,0:T(8,128)(2,1)S(1)}, u32[]{:S(2)}, u32[]{:S(2)}) async-start(bf16[8,16,1024]{2,1,0:T(8,128)(2,1)} %bitcast.57), calls=%async_computation | async-start | bytes 524288 | tf_op jit(solution)/shard_map/while/body/eval_jaxpr/all_to_all | solution.py:38
  405.4 60.9 %all-to-all-start = ((bf16[8,16,1024]{2,1,0:T(8,128)(2,1)}), bf16[8,16,1024]{2,1,0:T(8,128)(2,1)S(1)}, u32[]{:S(2)}, u32[]{:S(2)}) async-start(bf16[8,16,1024]{2,1,0:T(8,128)(2,1)} %bitcast.57), calls=%async_computation | async-start | bytes 524288 | tf_op jit(solution)/shard_map/while/body/eval_jaxpr/all_to_all | solution.py:38
  492.5 56.8 %all-reduce.2.cloned.1.call-start = ((), (), s32[]{:S(2)}) async-start(), calls=%async_computation.1 | async-start | bytes 524288 | tf_op jit(solution)/shard_map/while/body/eval_jaxpr/psum | solution.py:30
  500.6 60.9 %all-to-all-start = ((bf16[8,16,1024]{2,1,0:T(8,128)(2,1)}), bf16[8,16,1024]{2,1,0:T(8,128)(2,1)S(1)}, u32[]{:S(2)}, u32[]{:S(2)}) async-start(bf16[8,16,1024]{2,1,0:T(8,128)(2,1)} %bitcast.57), calls=%async_computation | async-start | bytes 524288 | tf_op jit(solution)/shard_map/while/body/eval_jaxpr/all_to_all | solution.py:38
  595.8 60.9 %all-to-all-start = ((bf16[8,16,1024]{2,1,0:T(8,128)(2,1)}), bf16[8,16,1024]{2,1,0:T(8,128)(2,1)S(1)}, u32[]{:S(2)}, u32[]{:S(2)}) async-start(bf16[8,16,1024]{2,1,0:T(8,128)(2,1)} %bitcast.57), calls=%async_computation | async-start | bytes 524288 | tf_op jit(solution)/shard_map/while/body/eval_jaxpr/all_to_all | solution.py:38
  691.0 60.9 %all-to-all-start = ((bf16[8,16,1024]{2,1,0:T(8,128)(2,1)}), bf16[8,16,1024]{2,1,0:T(8,128)(2,1)S(1)}, u32[]{:S(2)}, u32[]{:S(2)}) async-start(bf16[8,16,1024]{2,1,0:T(8,128)(2,1)} %bitcast.57), calls=%async_computation | async-start | bytes 524288 | tf_op jit(solution)/shard_map/while/body/eval_jaxpr/all_to_all | solution.py:38
  786.2 60.9 %all-to-all-start = ((bf16[8,16,1024]{2,1,0:T(8,128)(2,1)}), bf16[8,16,1024]{2,1,0:T(8,128)(2,1)S(1)}, u32[]{:S(2)}, u32[]{:S(2)}) async-start(bf16[8,16,1024]{2,1,0:T(8,128)(2,1)} %bitcast.57), calls=%async_computation | async-start | bytes 524288 | tf_op jit(solution)/shard_map/while/body/eval_jaxpr/all_to_all | solution.py:38
  873.3 56.8 %all-reduce.2.cloned.1.call-start = ((), (), s32[]{:S(2)}) async-start(), calls=%async_computation.1 | async-start | bytes 524288 | tf_op jit(solution)/shard_map/while/body/eval_jaxpr/psum | solution.py:30
  881.5 60.9 %all-to-all-start = ((bf16[8,16,1024]{2,1,0:T(8,128)(2,1)}), bf16[8,16,1024]{2,1,0:T(8,128)(2,1)S(1)}, u32[]{:S(2)}, u32[]{:S(2)}) async-start(bf16[8,16,1024]{2,1,0:T(8,128)(2,1)} %bitcast.57), calls=%async_computation | async-start | bytes 524288 | tf_op jit(solution)/shard_map/while/body/eval_jaxpr/all_to_all | solution.py:38
  968.6 56.8 %all-reduce.2.cloned.1.call-start = ((), (), s32[]{:S(2)}) async-start(), calls=%async_computation.1 | async-start | bytes 524288 | tf_op jit(solution)/shard_map/while/body/eval_jaxpr/psum | solution.py:30
  976.7 60.9 %all-to-all-start = ((bf16[8,16,1024]{2,1,0:T(8,128)(2,1)}), bf16[8,16,1024]{2,1,0:T(8,128)(2,1)S(1)}, u32[]{:S(2)}, u32[]{:S(2)}) async-start(bf16[8,16,1024]{2,1,0:T(8,128)(2,1)} %bitcast.57), calls=%async_computation | async-start | bytes 524288 | tf_op jit(solution)/shard_map/while/body/eval_jaxpr/all_to_all | solution.py:38
  1071.9 60.9 %all-to-all-start = ((bf16[8,16,1024]{2,1,0:T(8,128)(2,1)}), bf16[8,16,1024]{2,1,0:T(8,128)(2,1)S(1)}, u32[]{:S(2)}, u32[]{:S(2)}) async-start(bf16[8,16,1024]{2,1,0:T(8,128)(2,1)} %bitcast.57), calls=%async_computation | async-start | bytes 524288 | tf_op jit(solution)/shard_map/while/body/eval_jaxpr/all_to_all | solution.py:38
  1167.1 60.9 %all-to-all-start = ((bf16[8,16,1024]{2,1,0:T(8,128)(2,1)}), bf16[8,16,1024]{2,1,0:T(8,128)(2,1)S(1)}, u32[]{:S(2)}, u32[]{:S(2)}) async-start(bf16[8,16,1024]{2,1,0:T(8,128)(2,1)} %bitcast.57), calls=%async_computation | async-start | bytes 524288 | tf_op jit(solution)/shard_map/while/body/eval_jaxpr/all_to_all | solution.py:38
  1262.4 60.9 %all-to-all-start = ((bf16[8,16,1024]{2,1,0:T(8,128)(2,1)}), bf16[8,16,1024]{2,1,0:T(8,128)(2,1)S(1)}, u32[]{:S(2)}, u32[]{:S(2)}) async-start(bf16[8,16,1024]{2,1,0:T(8,128)(2,1)} %bitcast.57), calls=%async_computation | async-start | bytes 524288 | tf_op jit(solution)/shard_map/while/body/eval_jaxpr/all_to_all | solution.py:38
  1349.5 56.8 %all-reduce.2.cloned.1.call-start = ((), (), s32[]{:S(2)}) async-start(), calls=%async_computation.1 | async-start | bytes 524288 | tf_op jit(solution)/shard_map/while/body/eval_jaxpr/psum | solution.py:30
  1357.6 60.9 %all-to-all-start = ((bf16[8,16,1024]{2,1,0:T(8,128)(2,1)}), bf16[8,16,1024]{2,1,0:T(8,128)(2,1)S(1)}, u32[]{:S(2)}, u32[]{:S(2)}) async-start(bf16[8,16,1024]{2,1,0:T(8,128)(2,1)} %bitcast.57), calls=%async_computation | async-start | bytes 524288 | tf_op jit(solution)/shard_map/while/body/eval_jaxpr/all_to_all | solution.py:38
  1444.7 56.8 %all-reduce.2.cloned.1.call-start = ((), (), s32[]{:S(2)}) async-start(), calls=%async_computation.1 | async-start | bytes 524288 | tf_op jit(solution)/shard_map/while/body/eval_jaxpr/psum | solution.py:30
  1452.8 60.9 %all-to-all-start = ((bf16[8,16,1024]{2,1,0:T(8,128)(2,1)}), bf16[8,16,1024]{2,1,0:T(8,128)(2,1)S(1)}, u32[]{:S(2)}, u32[]{:S(2)}) async-start(bf16[8,16,1024]{2,1,0:T(8,128)(2,1)} %bitcast.57), calls=%async_computation | async-start | bytes 524288 | tf_op jit(solution)/shard_map/while/body/eval_jaxpr/all_to_all | solution.py:38
  1548.0 60.9 %all-to-all-start = ((bf16[8,16,1024]{2,1,0:T(8,128)(2,1)}), bf16[8,16,1024]{2,1,0:T(8,128)(2,1)S(1)}, u32[]{:S(2)}, u32[]{:S(2)}) async-start(bf16[8,16,1024]{2,1,0:T(8,128)(2,1)} %bitcast.57), calls=%async_computation | async-start | bytes 524288 | tf_op jit(solution)/shard_map/while/body/eval_jaxpr/all_to_all | solution.py:38
  1635.1 56.8 %all-reduce.2.cloned.1.call-start = ((), (), s32[]{:S(2)}) async-start(), calls=%async_computation.1 | async-start | bytes 524288 | tf_op jit(solution)/shard_map/while/body/eval_jaxpr/psum | solution.py:30
  1643.2 60.9 %all-to-all-start = ((bf16[8,16,1024]{2,1,0:T(8,128)(2,1)}), bf16[8,16,1024]{2,1,0:T(8,128)(2,1)S(1)}, u32[]{:S(2)}, u32[]{:S(2)}) async-start(bf16[8,16,1024]{2,1,0:T(8,128)(2,1)} %bitcast.57), calls=%async_computation | async-start | bytes 524288 | tf_op jit(solution)/shard_map/while/body/eval_jaxpr/all_to_all | solution.py:38
  1730.3 56.8 %all-reduce.2.cloned.1.call-start = ((), (), s32[]{:S(2)}) async-start(), calls=%async_computation.1 | async-start | bytes 524288 | tf_op jit(solution)/shard_map/while/body/eval_jaxpr/psum | solution.py:30
  1738.5 60.9 %all-to-all-start = ((bf16[8,16,1024]{2,1,0:T(8,128)(2,1)}), bf16[8,16,1024]{2,1,0:T(8,128)(2,1)S(1)}, u32[]{:S(2)}, u32[]{:S(2)}) async-start(bf16[8,16,1024]{2,1,0:T(8,128)(2,1)} %bitcast.57), calls=%async_computation | async-start | bytes 524288 | tf_op jit(solution)/shard_map/while/body/eval_jaxpr/all_to_all | solution.py:38
  1833.7 60.9 %all-to-all-start = ((bf16[8,16,1024]{2,1,0:T(8,128)(2,1)}), bf16[8,16,1024]{2,1,0:T(8,128)(2,1)S(1)}, u32[]{:S(2)}, u32[]{:S(2)}) async-start(bf16[8,16,1024]{2,1,0:T(8,128)(2,1)} %bitcast.57), calls=%async_computation | async-start | bytes 524288 | tf_op jit(solution)/shard_map/while/body/eval_jaxpr/all_to_all | solution.py:38
  1920.8 56.8 %all-reduce.2.cloned.1.call-start = ((), (), s32[]{:S(2)}) async-start(), calls=%async_computation.1 | async-start | bytes 524288 | tf_op jit(solution)/shard_map/while/body/eval_jaxpr/psum | solution.py:30
  1928.9 60.9 %all-to-all-start = ((bf16[8,16,1024]{2,1,0:T(8,128)(2,1)}), bf16[8,16,1024]{2,1,0:T(8,128)(2,1)S(1)}, u32[]{:S(2)}, u32[]{:S(2)}) async-start(bf16[8,16,1024]{2,1,0:T(8,128)(2,1)} %bitcast.57), calls=%async_computation | async-start | bytes 524288 | tf_op jit(solution)/shard_map/while/body/eval_jaxpr/all_to_all | solution.py:38
  2024.1 60.9 %all-to-all-start = ((bf16[8,16,1024]{2,1,0:T(8,128)(2,1)}), bf16[8,16,1024]{2,1,0:T(8,128)(2,1)S(1)}, u32[]{:S(2)}, u32[]{:S(2)}) async-start(bf16[8,16,1024]{2,1,0:T(8,128)(2,1)} %bitcast.57), calls=%async_computation | async-start | bytes 524288 | tf_op jit(solution)/shard_map/while/body/eval_jaxpr/all_to_all | solution.py:38
  2119.4 60.9 %all-to-all-start = ((bf16[8,16,1024]{2,1,0:T(8,128)(2,1)}), bf16[8,16,1024]{2,1,0:T(8,128)(2,1)S(1)}, u32[]{:S(2)}, u32[]{:S(2)}) async-start(bf16[8,16,1024]{2,1,0:T(8,128)(2,1)} %bitcast.57), calls=%async_computation | async-start | bytes 524288 | tf_op jit(solution)/shard_map/while/body/eval_jaxpr/all_to_all | solution.py:38
  2206.4 56.8 %all-reduce.2.cloned.1.call-start = ((), (), s32[]{:S(2)}) async-start(), calls=%async_computation.1 | async-start | bytes 524288 | tf_op jit(solution)/shard_map/while/body/eval_jaxpr/psum | solution.py:30
  2214.6 60.9 %all-to-all-start = ((bf16[8,16,1024]{2,1,0:T(8,128)(2,1)}), bf16[8,16,1024]{2,1,0:T(8,128)(2,1)S(1)}, u32[]{:S(2)}, u32[]{:S(2)}) async-start(bf16[8,16,1024]{2,1,0:T(8,128)(2,1)} %bitcast.57), calls=%async_computation | async-start | bytes 524288 | tf_op jit(solution)/shard_map/while/body/eval_jaxpr/all_to_all | solution.py:38
  2301.7 56.8 %all-reduce.2.cloned.1.call-start = ((), (), s32[]{:S(2)}) async-start(), calls=%async_computation.1 | async-start | bytes 524288 | tf_op jit(solution)/shard_map/while/body/eval_jaxpr/psum | solution.py:30
  2309.8 60.9 %all-to-all-start = ((bf16[8,16,1024]{2,1,0:T(8,128)(2,1)}), bf16[8,16,1024]{2,1,0:T(8,128)(2,1)S(1)}, u32[]{:S(2)}, u32[]{:S(2)}) async-start(bf16[8,16,1024]{2,1,0:T(8,128)(2,1)} %bitcast.57), calls=%async_computation | async-start | bytes 524288 | tf_op jit(solution)/shard_map/while/body/eval_jaxpr/all_to_all | solution.py:38
  2396.9 56.8 %all-reduce.2.cloned.1.call-start = ((), (), s32[]{:S(2)}) async-start(), calls=%async_computation.1 | async-start | bytes 524288 | tf_op jit(solution)/shard_map/while/body/eval_jaxpr/psum | solution.py:30
  2405.0 60.9 %all-to-all-start = ((bf16[8,16,1024]{2,1,0:T(8,128)(2,1)}), bf16[8,16,1024]{2,1,0:T(8,128)(2,1)S(1)}, u32[]{:S(2)}, u32[]{:S(2)}) async-start(bf16[8,16,1024]{2,1,0:T(8,128)(2,1)} %bitcast.57), calls=%async_computation | async-start | bytes 524288 | tf_op jit(solution)/shard_map/while/body/eval_jaxpr/all_to_all | solution.py:38
  2500.3 60.9 %all-to-all-start = ((bf16[8,16,1024]{2,1,0:T(8,128)(2,1)}), bf16[8,16,1024]{2,1,0:T(8,128)(2,1)S(1)}, u32[]{:S(2)}, u32[]{:S(2)}) async-start(bf16[8,16,1024]{2,1,0:T(8,128)(2,1)} %bitcast.57), calls=%async_computation | async-start | bytes 524288 | tf_op jit(solution)/shard_map/while/body/eval_jaxpr/all_to_all | solution.py:38
  2595.5 60.9 %all-to-all-start = ((bf16[8,16,1024]{2,1,0:T(8,128)(2,1)}), bf16[8,16,1024]{2,1,0:T(8,128)(2,1)S(1)}, u32[]{:S(2)}, u32[]{:S(2)}) async-start(bf16[8,16,1024]{2,1,0:T(8,128)(2,1)} %bitcast.57), calls=%async_computation | async-start | bytes 524288 | tf_op jit(solution)/shard_map/while/body/eval_jaxpr/all_to_all | solution.py:38
  2690.7 60.9 %all-to-all-start = ((bf16[8,16,1024]{2,1,0:T(8,128)(2,1)}), bf16[8,16,1024]{2,1,0:T(8,128)(2,1)S(1)}, u32[]{:S(2)}, u32[]{:S(2)}) async-start(bf16[8,16,1024]{2,1,0:T(8,128)(2,1)} %bitcast.57), calls=%async_computation | async-start | bytes 524288 | tf_op jit(solution)/shard_map/while/body/eval_jaxpr/all_to_all | solution.py:38
  2785.9 60.9 %all-to-all-start = ((bf16[8,16,1024]{2,1,0:T(8,128)(2,1)}), bf16[8,16,1024]{2,1,0:T(8,128)(2,1)S(1)}, u32[]{:S(2)}, u32[]{:S(2)}) async-start(bf16[8,16,1024]{2,1,0:T(8,128)(2,1)} %bitcast.57), calls=%async_computation | async-start | bytes 524288 | tf_op jit(solution)/shard_map/while/body/eval_jaxpr/all_to_all | solution.py:38
  2873.0 56.8 %all-reduce.2.cloned.1.call-start = ((), (), s32[]{:S(2)}) async-start(), calls=%async_computation.1 | async-start | bytes 524288 | tf_op jit(solution)/shard_map/while/body/eval_jaxpr/psum | solution.py:30
  2881.1 60.9 %all-to-all-start = ((bf16[8,16,1024]{2,1,0:T(8,128)(2,1)}), bf16[8,16,1024]{2,1,0:T(8,128)(2,1)S(1)}, u32[]{:S(2)}, u32[]{:S(2)}) async-start(bf16[8,16,1024]{2,1,0:T(8,128)(2,1)} %bitcast.57), calls=%async_computation | async-start | bytes 524288 | tf_op jit(solution)/shard_map/while/body/eval_jaxpr/all_to_all | solution.py:38
  2968.2 56.8 %all-reduce.2.cloned.1.call-start = ((), (), s32[]{:S(2)}) async-start(), calls=%async_computation.1 | async-start | bytes 524288 | tf_op jit(solution)/shard_map/while/body/eval_jaxpr/psum | solution.py:30
  2976.4 60.9 %all-to-all-start = ((bf16[8,16,1024]{2,1,0:T(8,128)(2,1)}), bf16[8,16,1024]{2,1,0:T(8,128)(2,1)S(1)}, u32[]{:S(2)}, u32[]{:S(2)}) async-start(bf16[8,16,1024]{2,1,0:T(8,128)(2,1)} %bitcast.57), calls=%async_computation | async-start | bytes 524288 | tf_op jit(solution)/shard_map/while/body/eval_jaxpr/all_to_all | solution.py:38
  (49 other events, 1274.6 us)
Sparse Core Ops, SparseCore 0:
  18.0 56.8 all-reduce.1
  117.1 51.2 all-reduce.1
  212.3 51.1 all-reduce.1
  307.5 51.2 all-reduce.1
  402.7 51.2 all-reduce.1
  498.0 51.2 all-reduce.1
  593.2 51.2 all-reduce.1
  688.4 51.2 all-reduce.1
  783.6 51.2 all-reduce.1
  878.8 51.2 all-reduce.1
  974.1 51.2 all-reduce.1
  1069.3 51.2 all-reduce.1
  1164.5 51.2 all-reduce.1
  1259.7 51.1 all-reduce.1
  1355.0 51.2 all-reduce.1
  1450.2 51.2 all-reduce.1
  1545.4 51.2 all-reduce.1
  1640.6 51.2 all-reduce.1
  1735.8 51.2 all-reduce.1
  1831.1 51.2 all-reduce.1
  1926.3 51.2 all-reduce.1
  2021.5 51.2 all-reduce.1
  2116.7 51.2 all-reduce.1
  2212.0 51.2 all-reduce.1
  2307.2 51.2 all-reduce.1
  2402.4 51.2 all-reduce.1
  2497.6 51.2 all-reduce.1
  2592.9 51.2 all-reduce.1
  2688.1 51.2 all-reduce.1
  2783.3 51.2 all-reduce.1
  2878.5 51.2 all-reduce.1
  2973.7 51.2 all-reduce.1
where the time goes:
time: 3100 us; the launch traced here: 3080 us
  waiting for transfers between devices  1450 us (47%)
  blocking collectives  519 us (17%)
  other arithmetic  448 us (14%)
  matrix products  365 us (12%)
  local copies, waits for them, and re-layouts  172 us (6%)
  starting transfers between devices  114 us (4%)
    psum x32, waiting for transfers between devices, micro_step(): tokens = lax.psum(partial_x, 'tp')  1450 us
    all_gather x32, blocking collectives, micro_step(): dx_all = lax.all_gather(d_x, 'tp', axis=0, tiled=True)  506 us
    scatter-add x32, other arithmetic, micro_step(): jax.ops.segment_sum(contrib, safe_ids, num_segments=rows_loc)  270 us
    dot_general x32, matrix products, micro_step(): lax.dot_general(normed, du_m, (((0,), (0,)), ((), ())), preferred_element...  203 us
    gather x32, local copies, waits for them, and re-layouts, micro_step(): looked = jnp.take(table_loc, safe_ids, axis=0)  121 us
    all_to_all x32, starting transfers between devices, micro_step(): lax.all_to_all(dn_part.reshape(group_size, seq_loc, model_dim), 'tp', 0,...  114 us
    dot_general x32, matrix products, micro_step(): lax.dot_general(du_m, w_loc, (((1,), (1,)), ((), ())), preferred_element_...  87.8 us
    dot_general x32, matrix products, micro_step(): jnp.dot(normed, w_loc, preferred_element_type=jnp.float32)  74.2 us
  transfers between devices with their start and end apart: 64, of which 32 were waited for; matrix products, arithmetic and copies ran while one was open for 15% of the time, Pallas kernels for 0%

commit v1 on v0

v1 whole, which is shorter than its diff:
```python
import functools
import jax
import jax.numpy as jnp
from jax import lax
from jax.experimental import pallas as pl
from jax.experimental.pallas import tpu as pltpu
from jax.sharding import PartitionSpec as P

NORM_EPS = 1e-6
LANES = 128
F32 = jnp.float32
BF16 = jnp.bfloat16
VMEM_MAX = 60 * 1024 * 1024


def _capacity(mean, slack):
    return -(-(mean * slack) // 128) * 128 // 8


def slow_step(token_ids, table_loc, gain_vec, w_loc, du_loc, dres_loc, group_size):
    seq_len = token_ids.shape[1]
    rows_loc, model_dim = table_loc.shape
    seq_loc = seq_len // group_size
    cols_loc = w_loc.shape[1]
    dev_idx = lax.axis_index('tp')
    row_start = dev_idx * rows_loc
    tok_start = dev_idx * seq_loc
    gain_f = gain_vec.astype(F32)

    def micro_step(acc_state, inputs):
        grad_table, grad_w, grad_gain = acc_state
        tok_ids, du_m, dres_m = inputs
        local_ids = tok_ids - row_start
        in_block = (local_ids >= 0) & (local_ids < rows_loc)
        safe_ids = jnp.where(in_block, local_ids, 0)
        looked = jnp.take(table_loc, safe_ids, axis=0)
        partial_x = jnp.where(in_block[:, None], looked, jnp.zeros_like(looked))
        tokens = lax.psum(partial_x, 'tp')
        tok_f = tokens.astype(F32)
        inv_rms = lax.rsqrt(jnp.mean(tok_f * tok_f, axis=-1, keepdims=True) + NORM_EPS)
        n_hat = tok_f * inv_rms
        normed = (n_hat * gain_f).astype(BF16)
        u_m = jnp.dot(normed, w_loc, preferred_element_type=F32).astype(BF16)
        x_own = lax.dynamic_slice_in_dim(tokens, tok_start, seq_loc, axis=0)
        dn_part = lax.dot_general(du_m, w_loc, (((1,), (1,)), ((), ())), preferred_element_type=F32).astype(BF16)
        dn_recv = lax.all_to_all(dn_part.reshape(group_size, seq_loc, model_dim), 'tp', 0, 0, tiled=True)
        d_norm = jnp.sum(dn_recv, axis=0, dtype=F32)
        hat_own = lax.dynamic_slice_in_dim(n_hat, tok_start, seq_loc, axis=0)
        inv_own = lax.dynamic_slice_in_dim(inv_rms, tok_start, seq_loc, axis=0)
        gain_dn = gain_f * d_norm
        centre = jnp.mean(hat_own * gain_dn, axis=-1, keepdims=True)
        d_x = (dres_m.astype(F32) + inv_own * (gain_dn - hat_own * centre)).astype(BF16)
        grad_gain = grad_gain + jnp.sum(d_norm * hat_own, axis=0)
        grad_w = grad_w + lax.dot_general(normed, du_m, (((0,), (0,)), ((), ())), preferred_element_type=F32)
        dx_all = lax.all_gather(d_x, 'tp', axis=0, tiled=True)
        contrib = jnp.where(in_block[:, None], dx_all.astype(F32), 0.0)
        grad_table = grad_table + jax.ops.segment_sum(contrib, safe_ids, num_segments=rows_loc)
        return (grad_table, grad_w, grad_gain), (u_m, x_own)

    init_state = (jnp.zeros((rows_loc, model_dim), F32), jnp.zeros((model_dim, cols_loc), F32), jnp.zeros((model_dim,), F32))
    (grad_table, grad_w, grad_gain), (u_proj, x_resid) = lax.scan(micro_step, init_state, (token_ids, du_loc, dres_loc))
    grad_gain = lax.psum(grad_gain, 'tp')
    return u_proj, x_resid, grad_table, grad_w, grad_gain


def index_tables(token_ids, rows_loc, group_size, cap, cap2):
    n_micro, seq_len = token_ids.shape
    seq_loc = seq_len // group_size
    per = n_micro * seq_loc
    me = lax.axis_index('tp')
    ids_h = token_ids.reshape(n_micro, group_size, seq_loc).transpose(1, 0, 2).reshape(group_size, per)
    owner = ids_h // rows_loc
    oh = owner[None] == jnp.arange(group_size, dtype=jnp.int32)[:, None, None]
    tri = (jnp.arange(per)[:, None] < jnp.arange(per)[None, :]).astype(BF16)
    ranks = jnp.dot(oh.reshape(group_size * group_size, per).astype(BF16), tri, preferred_element_type=F32)
    ranks = ranks.reshape(group_size, group_size, per).astype(jnp.int32)
    rk = jnp.sum(jnp.where(oh, ranks, 0), axis=0)
    cnt = jnp.sum(oh.astype(jnp.int32), axis=2)
    before = jnp.arange(group_size)[:, None] < jnp.arange(group_size)[None, :]
    base = jnp.sum(jnp.where(before[None], cnt[:, :, None], 0), axis=1)
    total = jnp.sum(cnt, axis=1)
    ok = (jnp.max(total) <= cap) & (jnp.max(cnt) <= cap2)
    grank = rk + jnp.sum(jnp.where(oh, base[:, :, None], 0), axis=0)
    gidx = owner * cap + jnp.minimum(grank, cap - 1)
    mine = jnp.where(owner == me, grank, -1).reshape(1, -1)
    row = (ids_h - me * rows_loc).reshape(1, -1)
    packid = jnp.sum(jnp.where(mine == jnp.arange(cap, dtype=jnp.int32)[:, None], row, 0), axis=1)
    slot2 = lax.dynamic_slice_in_dim(owner * cap2 + rk, me, 1, axis=0)
    inv2 = jnp.sum(jnp.where(slot2 == jnp.arange(group_size * cap2, dtype=jnp.int32)[:, None],
                             jnp.arange(per, dtype=jnp.int32)[None, :], 0), axis=1)
    base_me = lax.dynamic_slice_in_dim(base, me, 1, axis=0)[0]
    cnt_me = lax.dynamic_slice_in_dim(cnt, me, 1, axis=0)[0]
    return ok, gidx.reshape(-1), packid, inv2, base_me, cnt_me


def to_rows(dst, base, xf):
    r = xf.shape[0]
    for k in range(xf.shape[1] // LANES):
        dst[pl.ds(base * 8 + k, r, stride=8), :] = xf[:, k * LANES:(k + 1) * LANES]


def from_rows(src, base, r):
    return jnp.concatenate([src[pl.ds(base * 8 + k, r, stride=8), :] for k in range(8)], axis=1)


def gather_rows(dst, src, idx_ref, idx0, count, unroll=16):
    def body(i, c):
        for j in range(unroll):
            r = i * unroll + j
            s = pl.multiple_of(idx_ref[idx0 + r] * 8, 8)
            d = pl.multiple_of(r * 8, 8)
            dst[pl.ds(d, 8), :] = src[pl.ds(s, 8), :]
        return c
    lax.fori_loop(0, count // unroll, body, 0)


def norm_call(p_all, gidx, gain, cap, n_micro, group_size, seq_loc):
    n_rows, dim = p_all.shape
    per = n_micro * seq_loc
    sub = 64

    def kernel(gidx_ref, me_ref, p_ref, g_ref, n_ref, x_ref, land, rows, stage, sems):
        h = pl.program_id(0)

        @pl.when(h == 0)
        def _():
            def copy(o):
                return pltpu.make_async_copy(p_ref.at[pl.ds(o * cap, cap), :], land.at[o % 2], sems.at[o % 2])
            copy(0).start()
            for o in range(group_size):
                if o + 1 < group_size:
                    copy(o + 1).start()
                copy(o).wait()

                def body(c, carry):
                    off = pl.multiple_of(c * sub, sub)
                    to_rows(rows, o * cap + off, land[o % 2, pl.ds(off, sub), :].astype(F32))
                    return carry
                lax.fori_loop(0, cap // sub, body, 0)

        gather_rows(stage, rows, gidx_ref, h * per, per)
        gf = g_ref[...].astype(F32)
        for c in range(per // sub):
            xf = from_rows(stage, c * sub, sub)
            rs = lax.rsqrt(jnp.mean(xf * xf, axis=-1, keepdims=True) + NORM_EPS)
            nb = ((xf * rs) * gf).astype(BF16)
            m0 = c * sub // seq_loc
            ms = sub // seq_loc
            n_ref[pl.ds(m0, ms), 0, :, :] = nb.reshape(ms, seq_loc, dim)

            @pl.when(h == me_ref[0])
            def _():
                x_ref[pl.ds(m0, ms), :, :] = xf.astype(BF16).reshape(ms, seq_loc, dim)

    me = lax.axis_index('tp').astype(jnp.int32).reshape(1)
    return pl.pallas_call(
        kernel,
        grid_spec=pltpu.PrefetchScalarGridSpec(
            num_scalar_prefetch=2, grid=(group_size,),
            in_specs=[pl.BlockSpec(memory_space=pl.ANY), pl.BlockSpec((1, dim), lambda h, *_: (0, 0))],
            out_specs=[pl.BlockSpec((n_micro, 1, seq_loc, dim), lambda h, *_: (0, h, 0, 0)),
                       pl.BlockSpec((n_micro, seq_loc, dim), lambda h, *_: (0, 0, 0))],
            scratch_shapes=[pltpu.VMEM((2, cap, dim), BF16), pltpu.VMEM((n_rows * 8, LANES), F32),
                            pltpu.VMEM((per * 8, LANES), F32), pltpu.SemaphoreType.DMA((2,))]),
        out_shape=[jax.ShapeDtypeStruct((n_micro, group_size, seq_loc, dim), BF16),
                   jax.ShapeDtypeStruct((n_micro, seq_loc, dim), BF16)],
        compiler_params=pltpu.CompilerParams(dimension_semantics=("arbitrary",), vmem_limit_bytes=VMEM_MAX),
        cost_estimate=pl.CostEstimate(flops=12_000_000_000, bytes_accessed=18_000_000, transcendentals=0),
        name="norm_rows",
    )(gidx, me, p_all, gain.reshape(1, dim))


def dn_part_call(du4, w_loc):
    n_micro, group_size, seq_loc, cols = du4.shape
    dim = w_loc.shape[0]
    per = n_micro * seq_loc

    def kernel(du_ref, w_ref, o_ref):
        d = du_ref[...].reshape(per, cols)
        for c in range(0, dim, 256):
            o_ref[0, :, c:c + 256] = lax.dot_general(
                d, w_ref[c:c + 256, :], (((1,), (1,)), ((), ())), preferred_element_type=F32).astype(BF16)

    return pl.pallas_call(
        kernel, grid=(group_size,),
        in_specs=[pl.BlockSpec((n_micro, 1, seq_loc, cols), lambda h: (0, h, 0, 0)),
                  pl.BlockSpec((dim, cols), lambda h: (0, 0))],
        out_specs=pl.BlockSpec((1, per, dim), lambda h: (h, 0, 0)),
        out_shape=jax.ShapeDtypeStruct((group_size, per, dim), BF16),
        compiler_params=pltpu.CompilerParams(dimension_semantics=("arbitrary",), vmem_limit_bytes=VMEM_MAX),
        cost_estimate=pl.CostEstimate(flops=12_000_000_000, bytes_accessed=24_000_000, transcendentals=0),
        name="dn_part",
    )(du4, w_loc)


def dx_call(dn_recv, x_own, dres, gain, inv2):
    group_size, per, dim = dn_recv.shape
    n_micro, seq_loc, _ = x_own.shape
    slots = inv2.shape[0]
    sub = 64
    ms = sub // seq_loc
    steps = per // sub

    def kernel(inv_ref, dn_ref, x_ref, r_ref, g_ref, o_ref, dg_ref, rows, stage):
        c = pl.program_id(0)
        dn = dn_ref[0].astype(F32)
        for s in range(1, group_size):
            dn = dn + dn_ref[s].astype(F32)
        xf = x_ref[...].reshape(sub, dim).astype(F32)
        gf = g_ref[...].astype(F32)
        rs = lax.rsqrt(jnp.mean(xf * xf, axis=-1, keepdims=True) + NORM_EPS)
        nh = xf * rs
        gdn = gf * dn
        centre = jnp.mean(nh * gdn, axis=-1, keepdims=True)
        dx = (r_ref[...].reshape(sub, dim).astype(F32) + rs * (gdn - nh * centre)).astype(BF16)
        to_rows(rows, c * sub, dx.astype(F32))
        part = jnp.sum(dn * nh, axis=0, keepdims=True)

        @pl.when(c == 0)
        def _():
            dg_ref[...] = part

        @pl.when(c > 0)
        def _():
            dg_ref[...] += part

        @pl.when(c == steps - 1)
        def _():
            gather_rows(stage, rows, inv_ref, 0, slots)

            def body(i, carry):
                off = pl.multiple_of(i * sub, sub)
                o_ref[pl.ds(off, sub), :] = from_rows(stage, off, sub).astype(BF16)
                return carry
            lax.fori_loop(0, slots // sub, body, 0)

    return pl.pallas_call(
        kernel,
        grid_spec=pltpu.PrefetchScalarGridSpec(
            num_scalar_prefetch=1, grid=(steps,),
            in_specs=[pl.BlockSpec((group_size, sub, dim), lambda c, *_: (0, c, 0)),
                      pl.BlockSpec((ms, seq_loc, dim), lambda c, *_: (c, 0, 0)),
                      pl.BlockSpec((ms, seq_loc, dim), lambda c, *_: (c, 0, 0)),
                      pl.BlockSpec((1, dim), lambda c, *_: (0, 0))],
            out_specs=[pl.BlockSpec((slots, dim), lambda c, *_: (0, 0)),
                       pl.BlockSpec((1, dim), lambda c, *_: (0, 0))],
            scratch_shapes=[pltpu.VMEM((per * 8, LANES), F32), pltpu.VMEM((slots * 8, LANES), F32)]),
        out_shape=[jax.ShapeDtypeStruct((slots, dim), BF16), jax.ShapeDtypeStruct((1, dim), F32)],
        compiler_params=pltpu.CompilerParams(dimension_semantics=("arbitrary",), vmem_limit_bytes=VMEM_MAX),
        cost_estimate=pl.CostEstimate(flops=2_000_000_000, bytes_accessed=14_000_000, transcendentals=0),
        name="dx_rows",
    )(inv2, dn_recv, x_own, dres, gain.reshape(1, dim))


def table_grad_call(recv, packid, base_me, cnt_me, rows_loc, cap2):
    slots, dim = recv.shape
    group_size = slots // cap2
    sub = 64
    steps = 8
    blk = rows_loc // steps

    def kernel(id_ref, base_ref, cnt_ref, r_ref, o_ref, rows, acc):
        c = pl.program_id(0)

        @pl.when(c == 0)
        def _():
            def zero(i, carry):
                acc[pl.ds(pl.multiple_of(i * 512, 512), 512), :] = jnp.zeros((512, LANES), F32)
                return carry
            lax.fori_loop(0, rows_loc * 8 // 512, zero, 0)

            def conv(i, carry):
                off = pl.multiple_of(i * sub, sub)
                to_rows(rows, off, r_ref[pl.ds(off, sub), :].astype(F32))
                return carry
            lax.fori_loop(0, slots // sub, conv, 0)
            for h in range(group_size):
                b = base_ref[h]

                def add(r, carry):
                    t = pl.multiple_of(id_ref[b + r] * 8, 8)
                    s = pl.multiple_of((h * cap2 + r) * 8, 8)
                    acc[pl.ds(t, 8), :] += rows[pl.ds(s, 8), :]
                    return carry
                lax.fori_loop(0, cnt_ref[h], add, 0)

        for i in range(blk // sub):
            o_ref[i * sub:(i + 1) * sub, :] = from_rows(acc, c * blk + i * sub, sub)

    return pl.pallas_call(
        kernel,
        grid_spec=pltpu.PrefetchScalarGridSpec(
            num_scalar_prefetch=3, grid=(steps,),
            in_specs=[pl.BlockSpec((slots, dim), lambda c, *_: (0, 0))],
            out_specs=pl.BlockSpec((blk, dim), lambda c, *_: (c, 0)),
            scratch_shapes=[pltpu.VMEM((slots * 8, LANES), F32), pltpu.VMEM((rows_loc * 8, LANES), F32)]),
        out_shape=jax.ShapeDtypeStruct((rows_loc, dim), F32),
        compiler_params=pltpu.CompilerParams(dimension_semantics=("arbitrary",), vmem_limit_bytes=VMEM_MAX),
        cost_estimate=pl.CostEstimate(flops=2_000_000_000, bytes_accessed=12_000_000, transcendentals=0),
        name="table_grad",
    )(packid, base_me, cnt_me, recv)


def fast_step(tables, table_loc, gain_vec, w_loc, du_loc, dres_loc, group_size, cap, cap2):
    gidx, packid, inv2, base_me, cnt_me = tables
    n_micro, seq_len, cols = du_loc.shape
    seq_loc = seq_len // group_size
    rows_loc, dim = table_loc.shape
    du4 = du_loc.reshape(n_micro, group_size, seq_loc, cols)
    mine = jnp.take(table_loc, packid, axis=0)
    p_all = lax.all_gather(mine, 'tp', axis=0, tiled=True)
    dn_part = dn_part_call(du4, w_loc)
    dn_recv = lax.all_to_all(dn_part, 'tp', 0, 0, tiled=True)
    normed, x_own = norm_call(p_all, gidx, gain_vec, cap, n_micro, group_size, seq_loc)
    nt = normed.reshape(n_micro * seq_len, dim)
    u = jnp.dot(nt, w_loc, preferred_element_type=F32).astype(BF16)
    grad_w = lax.dot_general(nt, du_loc.reshape(n_micro * seq_len, cols), (((0,), (0,)), ((), ())), preferred_element_type=F32)
    dx_pack, dg = dx_call(dn_recv, x_own, dres_loc, gain_vec, inv2)
    recv = lax.all_to_all(dx_pack.reshape(group_size, cap2, dim), 'tp', 0, 0, tiled=True)
    grad_table = table_grad_call(recv.reshape(group_size * cap2, dim), packid, base_me, cnt_me, rows_loc, cap2)
    grad_gain = lax.psum(dg.reshape(dim), 'tp')
    return u.reshape(n_micro, seq_len, cols), x_own, grad_table, grad_w, grad_gain


def solution(mesh):
    group_size = mesh.shape['tp']

    def local_step(token_ids, table_loc, gain_vec, w_loc, du_loc, dres_loc):
        rows_loc = table_loc.shape[0]
        tokens = token_ids.shape[0] * token_ids.shape[1]
        cap = tokens // group_size * 5 // 4
        cap2 = tokens // group_size // group_size * 3 // 2
        ok, *tables = index_tables(token_ids, rows_loc, group_size, cap, cap2)
        return lax.cond(
            ok,
            lambda t, i, *a: fast_step(t, *a, group_size, cap, cap2),
            lambda t, i, *a: slow_step(i, *a, group_size),
            tuple(tables), token_ids, table_loc, gain_vec, w_loc, du_loc, dres_loc)

    return jax.shard_map(local_step, mesh=mesh,
                         in_specs=(P('dp', None), P('tp', None), P(None), P(None, 'tp'), P('dp', None, 'tp'), P('dp', 'tp', None)),
                         out_specs=(P('dp', None, 'tp'), P('dp', 'tp', None), P(('dp', 'tp'), None), P(None, ('dp', 'tp')), P('dp')),
                         check_vma=False)
```

time: 3100 us -> 253 us (0.08)
  waiting for transfers between devices: 1450 us -> 76.4 us
  blocking collectives: 519 us -> 13.2 us
  other arithmetic: 448 us -> 13.1 us
  matrix products: 365 us -> 38.4 us
  local copies, waits for them, and re-layouts: 172 us -> 17.5 us
  starting transfers between devices: 114 us -> 11.1 us
  Pallas kernels: 0 us -> 67 us
    psum x32 -> x0, waiting for transfers between devices: 1450 us -> none  [micro_step(): tokens = lax.psum(partial_x, 'tp')]
    all_gather x32 -> x0, blocking collectives: 506 us -> none  [micro_step(): dx_all = lax.all_gather(d_x, 'tp', axis=0, tiled=True)]
    dot_general x96 -> x3, matrix products: 365 us -> 38.4 us  [the longest x1 19.4 us: fast_step(): lax.dot_general(nt, du_loc.reshape(n_micro * seq_len, cols), (((0,), (0,)...]
    scatter-add x32 -> x0, other arithmetic: 270 us -> none  [micro_step(): jax.ops.segment_sum(contrib, safe_ids, num_segments=rows_loc)]
    gather x32 -> x1, local copies, waits for them, and re-layouts: 121 us -> 7.19 us  [fast_step(): mine = jnp.take(table_loc, packid, axis=0)]
    all_to_all x32 -> x2, starting transfers between devices: 114 us -> 10.9 us  [the longest x1 6.86 us: fast_step(): dn_recv = lax.all_to_all(dn_part, 'tp', 0, 0, tiled=True)]
    all_gather x0 -> x1, waiting for transfers between devices: none -> 73.6 us  [fast_step(): p_all = lax.all_gather(mine, 'tp', axis=0, tiled=True)]
    pallas_call x0 -> x4, Pallas kernels: none -> 67 us  [the longest x1 26.9 us: norm_call(): pl.pallas_call(kernel, grid_spec=pltpu.PrefetchScalarGridSpec(num_scalar_...]
  transfers between devices with their start and end apart: 64 -> 3, of which waited for: 32 -> 3; matrix products, arithmetic and copies ran while one was open for 15% -> 16% of each run, Pallas kernels for 0% -> 18%
where the time goes in v1:
time: 253 us; the launch traced here: 252 us
  waiting for transfers between devices  76.4 us (30%)
  Pallas kernels  67 us (26%)
  matrix products  38.4 us (15%)
  local copies, waits for them, and re-layouts  17.5 us (7%)
  between operations  15.5 us (6%)
  blocking collectives  13.2 us (5%)
  other arithmetic  13.1 us (5%)
  starting transfers between devices  11.1 us (4%)
    all_gather x1, waiting for transfers between devices, fast_step(): p_all = lax.all_gather(mine, 'tp', axis=0, tiled=True)  73.6 us
    pallas_call x1, Pallas kernels, norm_call(): pl.pallas_call(kernel, grid_spec=pltpu.PrefetchScalarGridSpec(num_scalar_...  26.9 us
    dot_general x1, matrix products, fast_step(): lax.dot_general(nt, du_loc.reshape(n_micro * seq_len, cols), (((0,), (0,)...  19.4 us
    dot_general x1, matrix products, fast_step(): u = jnp.dot(nt, w_loc, preferred_element_type=F32).astype(BF16)  18.7 us
    pallas_call x1, Pallas kernels, dn_part_call(): pl.pallas_call(kernel, grid=(group_size,), in_specs=[pl.BlockSpec((n_micr...  17.4 us
    psum x1, blocking collectives, slow_step(): grad_gain = lax.psum(grad_gain, 'tp')  13.2 us
    pallas_call x1, Pallas kernels, table_grad_call(): pl.pallas_call(kernel, grid_spec=pltpu.PrefetchScalarGridSpec(num_scalar_...  12.1 us
    pallas_call x1, Pallas kernels, dx_call(): pl.pallas_call(kernel, grid_spec=pltpu.PrefetchScalarGridSpec(num_scalar_...  10.6 us
  transfers between devices with their start and end apart: 3, of which 3 were waited for; matrix products, arithmetic and copies ran while one was open for 16% of the time, Pallas kernels for 18%

profile of v1, /device:TPU:81, one launch (start us, length us, event | category | flops | bytes accessed | tf_op | source)
XLA Modules:
  0.0 252.0 jit_solution(14735238535091770793)
XLA Ops:
  7.2 0.0 copy-start
  7.2 0.0 copy-start.4
  7.2 1.0 copy.15
  8.2 0.1 copy.16
  8.3 0.1 reshape.250
  8.4 0.1 reshape.249
  8.5 0.2 convert_reduce_fusion.1
  8.7 0.6 reduce_max.19
  10.0 0.1 select_reduce_fusion.3
  10.1 0.3 select_reduce_fusion.2
  10.4 0.6 reduce_max.18
  11.7 0.2 fusion.19
  12.0 1.3 broadcast_in_dim.149
  13.3 1.3 eq.63
  14.6 4.7 %eq.59 = s32[640,4096]{1,0:T(8,128)} iota(), iota_dimension=0 | iota | bytes 10485760 | tf_op jit(solution)/shard_map/eq | solution.py:87
  19.2 0.0 copy-done
  19.2 0.0 copy-done.4
  19.2 212.8 %conditional.1 = (bf16[32,128,1408]{2,1,0:T(8,128)(2,1)}, bf16[32,16,1024]{2,1,0:T(8,128)(2,1)}, f32[2048,1024]{1,0:T(8,128)}, f32[1024,1408]{1,0:T(8,128)}, f32[1024]{0:T(1024)S(1)}) conditional(s32[]{:T(128)} %convert_element_type.61, (bf16[1024]{0:T(1024)(128)(2,1)S(1)}, s32[32,128]{1,0:T(8,128)}, bf16[32,16,1024]{2,1,0:T(8,128)(2,1)}, ...), branch_computations={%region_9.19_spmd, %region_19.21_spmd} | conditional | flops 51637813248 | bytes 207140608 | solution.py:334
  19.3 0.2 all-gather.2.cloned.1.call-start
  19.5 0.6 compare_select_fusion
  20.1 5.3 %select_reduce_fusion.id_ref = s32[640]{0:T(1024)S(1)} fusion(s32[]{:T(128)} %get-tuple-element.274, s32[640,4096]{1,0:T(8,128)} %get-tuple-element.290, s32[4096]{0:T(1024)S(1)} %get-tuple-element.345, s32[]{:T(128)} %get-tuple-element.292, s32[4096]{0:T(1024)S(1)} %get-tuple-element.347), kind=kLoop, calls=%fused_computation.4 | loop fusion | flops 7863680 | bytes 10521096 | tf_op jit(solution)/shard_map/reduce_sum | solution.py:87
  25.4 0.0 copy-start.3
  25.5 7.2 %gather_fusion = bf16[640,1024]{1,0:T(8,128)(2,1)} fusion(bf16[2048,1024]{1,0:T(8,128)(2,1)} %get-tuple-element.206, s32[1024]{0:T(1024)S(1)} %pad_clamp_fusion), kind=kCustom, calls=%fused_computation.1 | custom fusion | bytes 2624000 | tf_op jit(solution)/shard_map/cond/branch_1_fun/jit(_take)/gather | solution.py:310
  32.6 2.6 %broadcast_select_fusion = bf16[640,1024]{1,0:T(8,128)(2,1)} fusion(bf16[640,1024]{1,0:T(8,128)(2,1)} %gather_fusion, pred[640]{0:T(1024)(128)(4,1)S(1)} %compare_and_fusion), kind=kLoop, calls=%fused_computation.6 | loop fusion | flops 655360 | bytes 2622080 | tf_op jit(solution)/shard_map/cond/branch_1_fun/jit(_take)/select_n | solution.py:310
  35.2 0.1 all-gather.2.cloned.1.call-update
  35.3 17.4 %dn_part.1 = bf16[8,512,1024]{2,1,0:T(8,128)(2,1)} custom-call(bf16[32,8,16,1408]{3,2,1,0:T(8,128)(2,1)} %bitcast.86, bf16[1024,1408]{1,0:T(8,128)(2,1)S(1)} %get-tuple-element.209.w_ref), custom_call_target="tpu_custom_call" | custom-call | flops 12000000000 | bytes 24000000 | tf_op jit(solution)/shard_map/cond/branch_1_fun/dn_part/pallas_call | solution.py:184
  52.6 0.0 copy-done.3
  52.6 6.9 %all-to-all-start = ((bf16[8,512,1024]{2,1,0:T(8,128)(2,1)}), bf16[8,512,1024]{2,1,0:T(8,128)(2,1)}, u32[]{:S(2)}, u32[]{:S(2)}) async-start(bf16[8,512,1024]{2,1,0:T(8,128)(2,1)} %dn_part.1), calls=%async_computation | async-start | bytes 16777216 | tf_op jit(solution)/shard_map/cond/branch_1_fun/all_to_all | solution.py:313
  59.5 0.6 reshape.237.g_ref
  60.1 2.7 %select_reduce_fusion.1.inv_ref = s32[768]{0:T(1024)} fusion(s32[]{:T(128)} %get-tuple-element.274, s32[768,512]{1,0:T(8,128)} %get-tuple-element.287, s32[768,512]{1,0:T(8,128)} %get-tuple-element.296, s32[512]{0:T(512)S(1)} %get-tuple-element.301, s32[]{:T(128)} %get-tuple-element.297), kind=kLoop, calls=%fused_computation.5 | loop fusion | flops 1178880 | bytes 3150856 | tf_op jit(solution)/shard_map/reduce_sum | solution.py:89
  62.8 73.6 %all-gather.2.cloned.1.call-done.p_ref = bf16[5120,1024]{1,0:T(8,128)(2,1)} async-done(((bf16[640,1024]{1,0:T(8,128)(2,1)}), bf16[5120,1024]{1,0:T(8,128)(2,1)}) %all-gather.2.cloned.1.call-update) | async-done | bytes 10485776 | tf_op jit(solution)/shard_map/cond/branch_1_fun/all_gather | solution.py:311
  136.4 26.9 %norm_rows.1 = (bf16[32,8,16,1024]{3,2,1,0:T(8,128)(2,1)}, bf16[32,16,1024]{2,1,0:T(8,128)(2,1)}) custom-call(s32[4096]{0:T(1024)} %get-tuple-element.346.gidx_ref, s32[1]{0:T(128)} %bitcast.me_ref, bf16[5120,1024]{1,0:T(8,128)(2,1)} %all-gather.2.cloned.1.call-done.p_ref, bf16[1,1024]{1,0:T(2,128)(2,1)} %reshape.237.g_ref), custom_call_target="tpu_custom_call" | custom-call | flops 12000000000 | bytes 18000000 | tf_op jit(solution)/shard_map/cond/branch_1_fun/norm_rows/pallas_call | solution.py:156
  163.3 18.7 %convolution_convert_fusion = bf16[4096,1408]{1,0:T(8,128)(2,1)} fusion(bf16[4096,1024]{1,0:T(8,128)(2,1)} %bitcast.94, bf16[1024,1408]{1,0:T(8,128)(2,1)S(1)} %get-tuple-element.209.w_ref), kind=kOutput, calls=%fused_computation.3 | convolution fusion | flops 11816927232 | bytes 22806528 | tf_op jit(solution)/shard_map/cond/branch_1_fun/dot_general | solution.py:316
  182.0 1.4 all-to-all-done.dn_ref
  183.5 10.6 %dx_rows.1 = (bf16[768,1024]{1,0:T(8,128)(2,1)}, f32[1,1024]{1,0:T(1,128)S(1)}) custom-call(s32[768]{0:T(1024)} %select_reduce_fusion.1.inv_ref, bf16[8,512,1024]{2,1,0:T(8,128)(2,1)} %all-to-all-done.dn_ref, bf16[32,16,1024]{2,1,0:T(8,128)(2,1)} %get-tuple-element.506.x_ref, bf16[32,16,1024]{2,1,0:T(8,128)(2,1)} %get-tuple-element.215.r_ref, ...), custom_call_target="tpu_custom_call" | custom-call | flops 2000000000 | bytes 14000000 | tf_op jit(solution)/shard_map/cond/branch_1_fun/dx_rows/pallas_call | solution.py:237
  194.1 4.0 %all-to-all-start.1 = ((bf16[8,96,1024]{2,1,0:T(8,128)(2,1)}), bf16[8,96,1024]{2,1,0:T(8,128)(2,1)S(1)}, u32[]{:S(2)}, u32[]{:S(2)}) async-start(bf16[8,96,1024]{2,1,0:T(8,128)(2,1)} %bitcast.85), calls=%async_computation.1 | async-start | bytes 3145728 | tf_op jit(solution)/shard_map/cond/branch_1_fun/all_to_all | solution.py:319
  198.1 19.4 %fusion.30 = f32[1024,1408]{1,0:T(8,128)} fusion(bf16[4096,1024]{1,0:T(8,128)(2,1)} %bitcast.95, bf16[4096,1408]{1,0:T(8,128)(2,1)} %bitcast.87), kind=kOutput, calls=%fused_computation.87 | convolution fusion | flops 11811160064 | bytes 25690112 | tf_op jit(solution)/shard_map/cond/branch_1_fun/dot_general | solution.py:317
  217.6 1.3 all-to-all-done.1
  218.8 0.0 copy-start.2
  218.8 1.1 copy-done.2
  220.0 12.1 %table_grad.1 = f32[2048,1024]{1,0:T(8,128)} custom-call(s32[640]{0:T(1024)} %copy-done.3, s32[8]{0:T(128)S(1)} %get-tuple-element.211.base_ref, s32[8]{0:T(128)S(1)} %get-tuple-element.212.cnt_ref, bf16[768,1024]{1,0:T(8,128)(2,1)} %bitcast.84), custom_call_target="tpu_custom_call" | custom-call | flops 2000000000 | bytes 12000000 | tf_op jit(solution)/shard_map/cond/branch_1_fun/table_grad/pallas_call | solution.py:290
  232.0 13.2 %psum.23 = f32[1024]{0:T(1024)} all-reduce(f32[1024]{0:T(1024)S(1)} %get-tuple-element.227), channel_id=1, replica_groups=mesh['dp'=4,'tp'=8] {'tp'}, use_global_device_ids=true, to_apply=%region_18.18 | all-reduce | flops 1024 | bytes 8192 | tf_op jit(solution)/shard_map/cond/branch_0_fun/psum | solution.py:62
  (11 shorter events, 0.1 us)
Async XLA Ops:
  7.2 12.1 %copy-start = (bf16[1024,1408]{1,0:T(8,128)(2,1)S(1)}, bf16[1024,1408]{1,0:T(8,128)(2,1)}, u32[]{:S(2)}) copy-start(bf16[1024,1408]{1,0:T(8,128)(2,1)} %param.13) | copy-start | bytes 8650756
  7.2 12.1 %copy-start.4 = (bf16[1024]{0:T(1024)(128)(2,1)S(1)}, bf16[1024]{0:T(1024)(128)(2,1)}, u32[]{:S(2)}) copy-start(bf16[1024]{0:T(1024)(128)(2,1)} %param.12) | copy-start | bytes 6148
  19.3 117.1 %all-gather.2.cloned.1.call-start = ((), (), s32[]{:S(2)}) async-start(), calls=%async_computation.3 | async-start | bytes 11796480 | tf_op jit(solution)/shard_map/cond/branch_1_fun/all_gather | solution.py:311
  25.4 27.2 %copy-start.3 = (s32[640]{0:T(1024)}, s32[640]{0:T(1024)S(1)}, u32[]{:S(2)}) copy-start(s32[640]{0:T(1024)S(1)} %select_reduce_fusion.id_ref) | copy-start | bytes 7684 | tf_op jit(solution)/shard_map/cond
  52.6 130.8 %all-to-all-start = ((bf16[8,512,1024]{2,1,0:T(8,128)(2,1)}), bf16[8,512,1024]{2,1,0:T(8,128)(2,1)}, u32[]{:S(2)}, u32[]{:S(2)}) async-start(bf16[8,512,1024]{2,1,0:T(8,128)(2,1)} %dn_part.1), calls=%async_computation | async-start | bytes 16777216 | tf_op jit(solution)/shard_map/cond/branch_1_fun/all_to_all | solution.py:313
  194.1 24.7 %all-to-all-start.1 = ((bf16[8,96,1024]{2,1,0:T(8,128)(2,1)}), bf16[8,96,1024]{2,1,0:T(8,128)(2,1)S(1)}, u32[]{:S(2)}, u32[]{:S(2)}) async-start(bf16[8,96,1024]{2,1,0:T(8,128)(2,1)} %bitcast.85), calls=%async_computation.1 | async-start | bytes 3145728 | tf_op jit(solution)/shard_map/cond/branch_1_fun/all_to_all | solution.py:319
  218.8 1.1 copy-start.2
Sparse Core Ops, SparseCore 0:
  35.4 100.9 all-gather.1

commit v2 on v0

v2 whole, which is shorter than its diff:
```python
import functools
import jax
import jax.numpy as jnp
from jax import lax
from jax.experimental import pallas as pl
from jax.experimental.pallas import tpu as pltpu
from jax.sharding import PartitionSpec as P

NORM_EPS = 1e-6
LANES = 128
F32 = jnp.float32
BF16 = jnp.bfloat16
VMEM_MAX = 60 * 1024 * 1024


def _capacity(mean, slack):
    return -(-(mean * slack) // 128) * 128 // 8


def slow_step(token_ids, table_loc, gain_vec, w_loc, du_loc, dres_loc, group_size):
    seq_len = token_ids.shape[1]
    rows_loc, model_dim = table_loc.shape
    seq_loc = seq_len // group_size
    cols_loc = w_loc.shape[1]
    dev_idx = lax.axis_index('tp')
    row_start = dev_idx * rows_loc
    tok_start = dev_idx * seq_loc
    gain_f = gain_vec.astype(F32)

    def micro_step(acc_state, inputs):
        grad_table, grad_w, grad_gain = acc_state
        tok_ids, du_m, dres_m = inputs
        local_ids = tok_ids - row_start
        in_block = (local_ids >= 0) & (local_ids < rows_loc)
        safe_ids = jnp.where(in_block, local_ids, 0)
        looked = jnp.take(table_loc, safe_ids, axis=0)
        partial_x = jnp.where(in_block[:, None], looked, jnp.zeros_like(looked))
        spread = lax.all_to_all(partial_x.reshape(group_size, seq_loc, model_dim), 'tp', 0, 0, tiled=True)
        mine = jnp.sum(spread, axis=0, dtype=F32).astype(BF16)
        tokens = lax.all_gather(mine, 'tp', axis=0, tiled=True)
        tok_f = tokens.astype(F32)
        inv_rms = lax.rsqrt(jnp.mean(tok_f * tok_f, axis=-1, keepdims=True) + NORM_EPS)
        n_hat = tok_f * inv_rms
        normed = (n_hat * gain_f).astype(BF16)
        u_m = jnp.dot(normed, w_loc, preferred_element_type=F32).astype(BF16)
        x_own = lax.dynamic_slice_in_dim(tokens, tok_start, seq_loc, axis=0)
        dn_part = lax.dot_general(du_m, w_loc, (((1,), (1,)), ((), ())), preferred_element_type=F32).astype(BF16)
        dn_recv = lax.all_to_all(dn_part.reshape(group_size, seq_loc, model_dim), 'tp', 0, 0, tiled=True)
        d_norm = jnp.sum(dn_recv, axis=0, dtype=F32)
        hat_own = lax.dynamic_slice_in_dim(n_hat, tok_start, seq_loc, axis=0)
        inv_own = lax.dynamic_slice_in_dim(inv_rms, tok_start, seq_loc, axis=0)
        gain_dn = gain_f * d_norm
        centre = jnp.mean(hat_own * gain_dn, axis=-1, keepdims=True)
        d_x = (dres_m.astype(F32) + inv_own * (gain_dn - hat_own * centre)).astype(BF16)
        grad_gain = grad_gain + jnp.sum(d_norm * hat_own, axis=0)
        grad_w = grad_w + lax.dot_general(normed, du_m, (((0,), (0,)), ((), ())), preferred_element_type=F32)
        dx_all = lax.all_gather(d_x, 'tp', axis=0, tiled=True)
        contrib = jnp.where(in_block[:, None], dx_all.astype(F32), 0.0)
        grad_table = grad_table + jax.ops.segment_sum(contrib, safe_ids, num_segments=rows_loc)
        return (grad_table, grad_w, grad_gain), (u_m, x_own)

    init_state = (jnp.zeros((rows_loc, model_dim), F32), jnp.zeros((model_dim, cols_loc), F32), jnp.zeros((model_dim,), F32))
    (grad_table, grad_w, grad_gain), (u_proj, x_resid) = lax.scan(micro_step, init_state, (token_ids, du_loc, dres_loc))
    grad_gain = lax.psum(grad_gain, 'tp')
    return u_proj, x_resid, grad_table, grad_w, grad_gain


def pack_call(token_ids, table_loc, group_size, cap, cap2):
    n_micro, seq_len = token_ids.shape
    seq_loc = seq_len // group_size
    per = n_micro * seq_loc
    rows_loc, dim = table_loc.shape
    slots = group_size * cap2
    pairs = group_size * group_size
    sub = 64
    ids_h = token_ids.reshape(n_micro, group_size, seq_loc).transpose(1, 0, 2).reshape(group_size, per)

    def kernel(ids_ref, e_ref, gidx_ref, pid_ref, inv_ref, stat_ref, p_ref, rows, stage, pid_s, sem):
        me = lax.axis_index('tp')
        ids = ids_ref[...]
        owner = ids // rows_loc
        oh = jnp.concatenate([(owner == o).astype(F32) for o in range(group_size)], axis=0)
        ohb = oh.astype(BF16)
        tri = (lax.broadcasted_iota(jnp.int32, (per, per), 0) < lax.broadcasted_iota(jnp.int32, (per, per), 1)).astype(F32).astype(BF16)
        rank = jnp.dot(ohb, tri, preferred_element_type=F32)
        nt = (((1,), (1,)), ((), ()))
        cnt_row = lax.dot_general(jnp.ones((8, per), BF16), ohb, nt, preferred_element_type=F32)[0:1]
        cnt_col = jnp.sum(oh, axis=1, keepdims=True)
        ra = lax.broadcasted_iota(jnp.int32, (pairs, pairs), 0)
        rb = lax.broadcasted_iota(jnp.int32, (pairs, pairs), 1)
        same = ra // group_size == rb // group_size
        base_col = jnp.sum(jnp.where(same & (rb < ra), cnt_row, 0.0), axis=1, keepdims=True)
        base_row = jnp.sum(jnp.where(same & (ra < rb), cnt_col, 0.0), axis=0, keepdims=True)
        tot_row = jnp.sum(jnp.where(same, cnt_col, 0.0), axis=0, keepdims=True)
        worst = jnp.concatenate([jnp.max(tot_row, axis=1, keepdims=True), jnp.max(cnt_row, axis=1, keepdims=True)], axis=0)

        def fold(v):
            s = v[0:group_size]
            for o in range(1, group_size):
                s = s + v[o * group_size:(o + 1) * group_size]
            return s.astype(jnp.int32)

        rk = fold(oh * rank)
        grank = fold(oh * (rank + base_col))
        gidx_ref[...] = owner * cap + jnp.minimum(grank, cap - 1)
        stat_ref[0:1, :] = cnt_row.astype(jnp.int32)
        stat_ref[1:2, :] = base_row.astype(jnp.int32)
        stat_ref[2:4, :] = jnp.broadcast_to(worst, (2, pairs)).astype(jnp.int32)
        stat_ref[4:8, :] = jnp.zeros((4, pairs), jnp.int32)

        def place(slot, value, n):
            hot = (slot == lax.broadcasted_iota(jnp.int32, (n, per), 0)).astype(F32).astype(BF16)
            parts = jnp.concatenate([value // 64, value % 64] + [jnp.zeros_like(value)] * 6, axis=0).astype(F32).astype(BF16)
            return lax.dot_general(parts, hot, nt, preferred_element_type=F32)

        mine = jnp.where(owner == me, grank, -1)
        local = jnp.clip(ids - me * rows_loc, 0, rows_loc - 1)
        acc = jnp.zeros((8, cap), F32)
        for h in range(group_size):
            acc = acc + place(mine[h:h + 1], local[h:h + 1], cap)
        pid = (acc[0:1] * 64.0 + acc[1:2]).astype(jnp.int32)
        pid_ref[...] = pid
        own = lax.broadcasted_iota(jnp.int32, (group_size, 1), 0) == me
        slot2 = jnp.sum(jnp.where(own, owner * cap2 + rk, 0), axis=0, keepdims=True)
        put = place(slot2, lax.broadcasted_iota(jnp.int32, (1, per), 1), slots)
        inv_ref[...] = (put[0:1] * 64.0 + put[1:2]).astype(jnp.int32)
        cp = pltpu.make_async_copy(pid_ref, pid_s, sem)
        cp.start()

        def conv(i, carry):
            off = pl.multiple_of(i * sub, sub)
            to_rows(rows, off, e_ref[pl.ds(off, sub), :].astype(F32))
            return carry
        lax.fori_loop(0, rows_loc // sub, conv, 0)
        cp.wait()
        gather_rows(stage, rows, lambda r: pid_s[0, r], cap)

        def back(i, carry):
            off = pl.multiple_of(i * sub, sub)
            p_ref[pl.ds(off, sub), :] = from_rows(stage, off, sub).astype(BF16)
            return carry
        lax.fori_loop(0, cap // sub, back, 0)

    vspec = pl.BlockSpec(memory_space=pltpu.VMEM)
    return pl.pallas_call(
        kernel,
        in_specs=[vspec, vspec],
        out_specs=[vspec] * 5,
        out_shape=[jax.ShapeDtypeStruct((group_size, per), jnp.int32),
                   jax.ShapeDtypeStruct((1, cap), jnp.int32),
                   jax.ShapeDtypeStruct((1, slots), jnp.int32),
                   jax.ShapeDtypeStruct((8, pairs), jnp.int32),
                   jax.ShapeDtypeStruct((cap, dim), BF16)],
        scratch_shapes=[pltpu.VMEM((rows_loc, 8, LANES), F32), pltpu.VMEM((cap, 8, LANES), F32),
                        pltpu.SMEM((1, cap), jnp.int32), pltpu.SemaphoreType.DMA(())],
        compiler_params=pltpu.CompilerParams(vmem_limit_bytes=VMEM_MAX),
        name="pack_rows",
    )(ids_h, table_loc)


def flat(ref):
    return ref.reshape(ref.shape[0] * 8, LANES)


def to_rows(dst, base, xf):
    r = xf.shape[0]
    for k in range(8):
        flat(dst)[pl.ds(base * 8 + k, r, stride=8), :] = xf[:, k * LANES:(k + 1) * LANES]


def from_rows(src, base, r):
    return jnp.concatenate([flat(src)[pl.ds(base * 8 + k, r, stride=8), :] for k in range(8)], axis=1)


def gather_rows(dst, src, index, count, unroll=16):
    def body(i, c):
        for j in range(unroll):
            r = i * unroll + j
            dst[r] = src[index(r)]
        return c
    lax.fori_loop(0, count // unroll, body, 0)


def group_call(p_own, gidx, inv2, gain, w_loc, du4, dres, cap, cap2):
    n_micro, group_size, seq_loc, cols = du4.shape
    chips = group_size // 2
    dim = w_loc.shape[0]
    per = n_micro * seq_loc
    half = per // 2
    piece = half // 2
    hcap = cap // 2
    slots = group_size * cap2
    sub = 64
    far = chips // 2

    def kernel(gidx_ref, inv_ref, p_ref, g_ref, w_ref, du_ref, r_ref,
               pall_ref, n_ref, x_ref, pack_ref, dg_ref, dw_ref,
               rows, land, stage, nbuf, ntr, dub, part, relay_in, relay_p, relay_out,
               own_p, direct, summed, dg_all, land_sem, du_sem, n_sem, send, recv):
        me = lax.axis_index('tp')
        c = me // 2
        k = me % 2

        def dev(chip_off, core):
            return ((c + chip_off) % chips) * 2 + core

        right, left, partner = dev(1, k), dev(chips - 1, k), dev(0, 1 - k)
        barrier = pltpu.get_barrier_semaphore()
        for o in range(1, group_size):
            pl.semaphore_signal(barrier, inc=1, device_id={'tp': (me + o) % group_size}, device_id_type=pl.DeviceIdType.MESH)
        pl.semaphore_wait(barrier, group_size - 1)

        def rcopy(src, dst, s, r, to):
            return pltpu.make_async_remote_copy(src_ref=src, dst_ref=dst, send_sem=send.at[s], recv_sem=recv.at[r],
                                                device_id={'tp': to}, device_id_type=pl.DeviceIdType.MESH)

        def arrived(dst, r):
            pltpu.make_async_remote_copy(src_ref=dst, dst_ref=dst, send_sem=send.at[0], recv_sem=recv.at[r],
                                         device_id={'tp': partner}, device_id_type=pl.DeviceIdType.MESH).wait_recv()

        sent = []

        def go(cp):
            cp.start()
            sent.append(cp)

        def blk(d, off=0, n=cap):
            return pall_ref.at[pl.ds(pl.multiple_of(d * cap + off, 16), n), :]

        go(rcopy(p_ref, blk(me), 0, 0, right))
        go(rcopy(p_ref, blk(me), 1, 1, left))
        go(rcopy(p_ref, blk(me), 2, 2, partner))

        def du_copy(d, slot):
            return pltpu.make_async_copy(du_ref.at[:, d], dub.at[slot], du_sem.at[slot])

        def order(j):
            return ((c + far + j // 2) % chips) * 2 + j % 2

        du_copy(order(0), 0).start()

        def dn_body(j, carry):
            slot = j % 2

            @pl.when(j + 1 < group_size)
            def _():
                du_copy(order(j + 1), 1 - slot).start()
            du_copy(order(j), slot).wait()
            d = order(j)
            dv = dub[slot].reshape(per, cols)
            for t in range(0, dim, 256):
                part[d, :, t:t + 256] = lax.dot_general(
                    dv, w_ref[t:t + 256, :], (((1,), (1,)), ((), ())), preferred_element_type=F32).astype(BF16)
            return carry
        lax.fori_loop(0, group_size, dn_body, 0)

        du_copy(0, 0).start()

        def first_hop(kk):
            d = dev(far, kk)
            go(rcopy(part.at[d, pl.ds(0, half)], relay_in.at[0, k], 9 + kk, 9 + k, dev(chips - 1, kk)))
            go(rcopy(part.at[d, pl.ds(half, half)], relay_in.at[1, k], 11 + kk, 11 + k, dev(1, kk)))

        first_hop(0)
        dl, dr = dev(chips - 1, 1 - k), dev(1, 1 - k)
        go(rcopy(part.at[dl, pl.ds(0, half)], relay_p.at[0], 17, 17, partner))
        go(rcopy(part.at[dr, pl.ds(half, half)], relay_p.at[1], 18, 18, partner))
        go(rcopy(part.at[partner], own_p, 19, 19, partner))

        def convert(src, base, n):
            cp = pltpu.make_async_copy(src, land.at[pl.ds(0, n), :], land_sem)
            cp.start()
            cp.wait()

            def body(i, carry):
                off = pl.multiple_of(i * sub, sub)
                to_rows(rows, base + off, land[pl.ds(off, sub), :].astype(F32))
                return carry
            lax.fori_loop(0, n // sub, body, 0)

        convert(p_ref, me * cap, cap)
        arrived(blk(partner), 2)
        convert(blk(partner), partner * cap, cap)

        arrived(blk(left), 0)
        go(rcopy(blk(left, 0, hcap), blk(left, 0, hcap), 3, 3, right))
        arrived(blk(right), 1)
        go(rcopy(blk(right, hcap, hcap), blk(right, hcap, hcap), 4, 4, left))
        go(rcopy(blk(left), blk(left), 5, 5, partner))
        go(rcopy(blk(right), blk(right), 6, 6, partner))
        first_hop(1)
        for kk in range(2):
            go(rcopy(part.at[dev(chips - 1, kk), pl.ds(half, half)], direct.at[1, k], 13 + kk, 13 + k, dev(chips - 1, kk)))
            go(rcopy(part.at[dev(1, kk), pl.ds(0, half)], direct.at[0, k], 15 + kk, 15 + k, dev(1, kk)))
        convert(blk(left), left * cap, cap)
        convert(blk(right), right * cap, cap)
        pl_, pr_ = dev(chips - 1, 1 - k), dev(1, 1 - k)
        arrived(blk(pl_), 5)
        convert(blk(pl_), pl_ * cap, cap)
        arrived(blk(pr_), 6)
        convert(blk(pr_), pr_ * cap, cap)
        fk, fp = dev(far, k), dev(far, 1 - k)
        arrived(blk(fk, 0, hcap), 3)
        go(rcopy(blk(fk, 0, hcap), blk(fk, 0, hcap), 7, 7, partner))
        arrived(blk(fk, hcap, hcap), 4)
        go(rcopy(blk(fk, hcap, hcap), blk(fk, hcap, hcap), 8, 8, partner))
        convert(blk(fk), fk * cap, cap)
        arrived(blk(fp, 0, hcap), 7)
        arrived(blk(fp, hcap, hcap), 8)
        convert(blk(fp), fp * cap, cap)

        relays = [[rcopy(relay_out.at[s, pl.ds(q * piece, piece)], summed.at[s, pl.ds(q * piece, piece)],
                         20 + 2 * s + q, 20 + 2 * s + q, left if s == 0 else right) for q in range(2)] for s in range(2)]

        def relay():
            for s in range(2):
                d = left if s == 0 else right
                arrived(relay_p.at[s], 17 + s)
                for kk in range(2):
                    arrived(relay_in.at[s, kk], 9 + 2 * s + kk)
                for q in range(2):
                    def body(i, carry):
                        o = pl.multiple_of(q * piece + i * sub, sub)
                        a = part[d, pl.ds(pl.multiple_of(s * half + o, sub), sub), :].astype(F32)
                        a = a + relay_p[s, pl.ds(o, sub), :].astype(F32)
                        a = a + relay_in[s, 0, pl.ds(o, sub), :].astype(F32)
                        a = a + relay_in[s, 1, pl.ds(o, sub), :].astype(F32)
                        relay_out[s, pl.ds(o, sub), :] = a
                        return carry
                    lax.fori_loop(0, piece // sub, body, 0)
            for q in range(2):
                for s in range(2):
                    relays[s][q].start()

        gf = g_ref[...].astype(F32)

        def n_copy(h, slot):
            return pltpu.make_async_copy(nbuf.at[slot], n_ref.at[:, h], n_sem.at[slot])

        def chunk(h, carry):
            slot = h % 2

            @pl.when(h == 2)
            def _():
                relay()

            @pl.when(h + 1 < group_size)
            def _():
                du_copy(h + 1, 1 - slot).start()
            gather_rows(stage, rows, lambda r: gidx_ref[h, r], per)

            @pl.when(h >= 2)
            def _():
                n_copy(h - 2, slot).wait()

            def norm(i, carry2):
                off = pl.multiple_of(i * sub, sub)
                ms = sub // seq_loc
                xf = from_rows(stage, off, sub)
                rs = lax.rsqrt(jnp.mean(xf * xf, axis=-1, keepdims=True) + NORM_EPS)
                nb = ((xf * rs) * gf).astype(BF16)
                nbuf[slot, pl.ds(i * ms, ms)] = nb.reshape(ms, seq_loc, dim)

                @pl.when(h == me)
                def _():
                    x_ref[pl.ds(i * ms, ms)] = xf.astype(BF16).reshape(ms, seq_loc, dim)
                return carry2
            lax.fori_loop(0, per // sub, norm, 0)
            n_copy(h, slot).start()
            ntr[...] = nbuf[slot].reshape(per, dim).T
            du_copy(h, slot).wait()
            for t in range(0, cols, 256):
                w = min(256, cols - t)
                dv = dub[slot, :, :, t:t + w].reshape(per, w)
                contrib = jnp.dot(ntr[...], dv, preferred_element_type=F32)

                @pl.when(h == 0)
                def _():
                    dw_ref[:, t:t + w] = contrib

                @pl.when(h > 0)
                def _():
                    dw_ref[:, t:t + w] += contrib
            return carry
        lax.fori_loop(0, group_size, chunk, 0)
        n_copy(group_size - 2, 0).wait()
        n_copy(group_size - 1, 1).wait()

        arrived(own_p, 19)
        for kk in range(2):
            arrived(direct.at[0, kk], 15 + kk)
            arrived(direct.at[1, kk], 13 + kk)
        for q in range(2):
            for s in range(2):
                arrived(summed.at[s, pl.ds(q * piece, piece)], 20 + 2 * s + q)

                def body(i, acc):
                    ms = sub // seq_loc
                    o = pl.multiple_of(q * piece + i * sub, sub)
                    f = pl.multiple_of(s * half + o, sub)
                    dn = summed[s, pl.ds(o, sub), :] + part[me, pl.ds(f, sub), :].astype(F32)
                    dn = dn + own_p[pl.ds(f, sub), :].astype(F32)
                    dn = dn + direct[s, 0, pl.ds(o, sub), :].astype(F32)
                    dn = dn + direct[s, 1, pl.ds(o, sub), :].astype(F32)
                    m0 = f // seq_loc
                    xf = x_ref[pl.ds(m0, ms)].reshape(sub, dim).astype(F32)
                    rs = lax.rsqrt(jnp.mean(xf * xf, axis=-1, keepdims=True) + NORM_EPS)
                    nh = xf * rs
                    gdn = gf * dn
                    centre = jnp.mean(nh * gdn, axis=-1, keepdims=True)
                    dres_f = r_ref[pl.ds(m0, ms)].reshape(sub, dim).astype(F32)
                    dx = (dres_f + rs * (gdn - nh * centre)).astype(BF16)
                    to_rows(stage, f, dx.astype(F32))
                    return acc + jnp.sum(dn * nh, axis=0, keepdims=True)
                got = lax.fori_loop(0, piece // sub, body, jnp.zeros((1, dim), F32))
                if q == 0 and s == 0:
                    dg_all[me] = got
                else:
                    dg_all[me] += got

        for o in range(1, group_size):
            go(rcopy(dg_all.at[me], dg_all.at[me], 23 + o, 23 + o, (me + o) % group_size))
        gather_rows(rows, stage, lambda r: inv_ref[0, r], slots)

        def out(i, carry):
            off = pl.multiple_of(i * sub, sub)
            pack_ref[pl.ds(off, sub), :] = from_rows(rows, off, sub).astype(BF16)
            return carry
        lax.fori_loop(0, slots // sub, out, 0)
        for o in range(1, group_size):
            arrived(dg_all.at[(me + group_size - o) % group_size], 23 + o)
        dg = dg_all[0]
        for o in range(1, group_size):
            dg = dg + dg_all[o]
        dg_ref[...] = dg
        for cp in sent:
            cp.wait_send()
        for s in range(2):
            for q in range(2):
                relays[s][q].wait_send()

    anyspec = pl.BlockSpec(memory_space=pl.ANY)
    vspec = pl.BlockSpec(memory_space=pltpu.VMEM)
    sspec = pl.BlockSpec(memory_space=pltpu.SMEM)
    return pl.pallas_call(
        kernel,
        in_specs=[sspec, sspec, anyspec, vspec, vspec, anyspec, vspec],
        out_specs=[anyspec, anyspec, vspec, vspec, vspec, vspec],
        out_shape=[jax.ShapeDtypeStruct((group_size * cap, dim), BF16),
                   jax.ShapeDtypeStruct((n_micro, group_size, seq_loc, dim), BF16),
                   jax.ShapeDtypeStruct((n_micro, seq_loc, dim), BF16),
                   jax.ShapeDtypeStruct((slots, dim), BF16),
                   jax.ShapeDtypeStruct((1, dim), F32),
                   jax.ShapeDtypeStruct((dim, cols), F32)],
        scratch_shapes=[pltpu.VMEM((group_size * cap, 8, LANES), F32),
                        pltpu.VMEM((cap, dim), BF16),
                        pltpu.VMEM((per, 8, LANES), F32),
                        pltpu.VMEM((2, n_micro, seq_loc, dim), BF16),
                        pltpu.VMEM((dim, per), BF16),
                        pltpu.VMEM((2, n_micro, seq_loc, cols), BF16),
                        pltpu.VMEM((group_size, per, dim), BF16),
                        pltpu.VMEM((2, 2, half, dim), BF16),
                        pltpu.VMEM((2, half, dim), BF16),
                        pltpu.VMEM((2, half, dim), F32),
                        pltpu.VMEM((per, dim), BF16),
                        pltpu.VMEM((2, 2, half, dim), BF16),
                        pltpu.VMEM((2, half, dim), F32),
                        pltpu.VMEM((group_size, 1, dim), F32),
                        pltpu.SemaphoreType.DMA(()),
                        pltpu.SemaphoreType.DMA((2,)),
                        pltpu.SemaphoreType.DMA((2,)),
                        pltpu.SemaphoreType.DMA((32,)),
                        pltpu.SemaphoreType.DMA((32,))],
        compiler_params=pltpu.CompilerParams(collective_id=0, has_side_effects=True, vmem_limit_bytes=66_900_000),
        name="group_rows",
    )(gidx, inv2, p_own, gain.reshape(1, dim), w_loc, du4, dres)


def table_grad_call(recv, packid, stat, rows_loc, cap2):
    slots, dim = recv.shape
    group_size = slots // cap2
    sub = 64
    steps = 8
    blk = rows_loc // steps

    def kernel(id_ref, stat_ref, r_ref, o_ref, rows, acc):
        c = pl.program_id(0)
        first = lax.axis_index('tp') * group_size

        @pl.when(c == 0)
        def _():
            def zero(i, carry):
                acc[pl.ds(i * sub, sub)] = jnp.zeros((sub, 8, LANES), F32)
                return carry
            lax.fori_loop(0, rows_loc // sub, zero, 0)

            def conv(i, carry):
                off = pl.multiple_of(i * sub, sub)
                to_rows(rows, off, r_ref[pl.ds(off, sub), :].astype(F32))
                return carry
            lax.fori_loop(0, slots // sub, conv, 0)
            for h in range(group_size):
                b = stat_ref[1, first + h]

                def add(r, carry):
                    t = id_ref[0, b + r]
                    acc[t] += rows[h * cap2 + r]
                    return carry
                lax.fori_loop(0, stat_ref[0, first + h], add, 0)

        for i in range(blk // sub):
            o_ref[i * sub:(i + 1) * sub, :] = from_rows(acc, c * blk + i * sub, sub)

    return pl.pallas_call(
        kernel,
        grid_spec=pltpu.PrefetchScalarGridSpec(
            num_scalar_prefetch=2, grid=(steps,),
            in_specs=[pl.BlockSpec((slots, dim), lambda c, *_: (0, 0))],
            out_specs=pl.BlockSpec((blk, dim), lambda c, *_: (c, 0)),
            scratch_shapes=[pltpu.VMEM((slots, 8, LANES), F32), pltpu.VMEM((rows_loc, 8, LANES), F32)]),
        out_shape=jax.ShapeDtypeStruct((rows_loc, dim), F32),
        compiler_params=pltpu.CompilerParams(dimension_semantics=("arbitrary",), vmem_limit_bytes=VMEM_MAX),
        cost_estimate=pl.CostEstimate(flops=2_000_000_000, bytes_accessed=12_000_000, transcendentals=0),
        name="table_grad",
    )(packid, stat, recv)


def fast_step(tables, table_loc, gain_vec, w_loc, du_loc, dres_loc, group_size, cap, cap2):
    gidx, packid, inv2, stat, mine = tables
    n_micro, seq_len, cols = du_loc.shape
    seq_loc = seq_len // group_size
    rows_loc, dim = table_loc.shape
    du4 = du_loc.reshape(n_micro, group_size, seq_loc, cols)
    _, normed, x_own, dx_pack, dg, grad_w = group_call(mine, gidx, inv2, gain_vec, w_loc, du4, dres_loc, cap, cap2)
    nt = normed.reshape(n_micro * seq_len, dim)
    u = jnp.dot(nt, w_loc, preferred_element_type=F32).astype(BF16)
    recv = lax.all_to_all(dx_pack.reshape(group_size, cap2, dim), 'tp', 0, 0, tiled=True)
    grad_table = table_grad_call(recv.reshape(group_size * cap2, dim), packid, stat, rows_loc, cap2)
    grad_gain = dg.reshape(dim)
    return u.reshape(n_micro, seq_len, cols), x_own, grad_table, grad_w, grad_gain


def solution(mesh):
    group_size = mesh.shape['tp']

    def local_step(token_ids, table_loc, gain_vec, w_loc, du_loc, dres_loc):
        rows_loc = table_loc.shape[0]
        tokens = token_ids.shape[0] * token_ids.shape[1]
        cap = tokens // group_size * 5 // 4
        cap2 = tokens // group_size // group_size * 3 // 2
        tables = pack_call(token_ids, table_loc, group_size, cap, cap2)
        ok = (tables[3][2, 0] <= cap) & (tables[3][3, 0] <= cap2)
        return lax.cond(
            ok,
            lambda t, i, *a: fast_step(t, *a, group_size, cap, cap2),
            lambda t, i, *a: slow_step(i, *a, group_size),
            tuple(tables), token_ids, table_loc, gain_vec, w_loc, du_loc, dres_loc)

    return jax.shard_map(local_step, mesh=mesh,
                         in_specs=(P('dp', None), P('tp', None), P(None), P(None, 'tp'), P('dp', None, 'tp'), P('dp', 'tp', None)),
                         out_specs=(P('dp', None, 'tp'), P('dp', 'tp', None), P(('dp', 'tp'), None), P(None, ('dp', 'tp')), P('dp')),
                         check_vma=False)
```

time: 3100 us -> 200 us (0.06)
  waiting for transfers between devices: 1450 us -> 1.62 us
  blocking collectives: 519 us -> 0 us
  other arithmetic: 448 us -> 0 us
  matrix products: 365 us -> 19.1 us
  Pallas kernels: 0 us -> 159 us
  local copies, waits for them, and re-layouts: 172 us -> 13 us
  starting transfers between devices: 114 us -> 3.9 us
    psum x32 -> x0, waiting for transfers between devices: 1450 us -> none  [micro_step(): tokens = lax.psum(partial_x, 'tp')]
    all_gather x32 -> x0, blocking collectives: 506 us -> none  [micro_step(): dx_all = lax.all_gather(d_x, 'tp', axis=0, tiled=True)]
    dot_general x96 -> x1, matrix products: 365 us -> 19.1 us  [fast_step(): u = jnp.dot(nt, w_loc, preferred_element_type=F32).astype(BF16)]
    scatter-add x32 -> x0, other arithmetic: 270 us -> none  [micro_step(): jax.ops.segment_sum(contrib, safe_ids, num_segments=rows_loc)]
    pallas_call x0 -> x3, Pallas kernels: none -> 159 us  [the longest x1 139 us: group_call(): pl.pallas_call(kernel, in_specs=[sspec, sspec, anyspec, vspec, vspec, any...]
    gather x32 -> x0, local copies, waits for them, and re-layouts: 121 us -> none  [micro_step(): looked = jnp.take(table_loc, safe_ids, axis=0)]
    all_to_all x32 -> x1, starting transfers between devices: 114 us -> 3.9 us  [fast_step(): lax.all_to_all(dx_pack.reshape(group_size, cap2, dim), 'tp', 0, 0, tiled=...]
    reduce_sum x96 -> x0, other arithmetic: 69.6 us -> none  [the longest x32 36.9 us: micro_step(): jnp.mean(tok_f * tok_f, axis=-1, keepdims=True) + NORM_EPS]
  transfers between devices with their start and end apart: 64 -> 1, of which waited for: 32 -> 1; matrix products, arithmetic and copies ran while one was open for 15% -> 10% of each run, Pallas kernels for 0% -> 0%
where the time goes in v2:
time: 200 us; the launch traced here: 199 us
  Pallas kernels  159 us (80%)
  matrix products  19.1 us (10%)
  local copies, waits for them, and re-layouts  13 us (6%)
  starting transfers between devices  3.9 us (2%)
    pallas_call x1, Pallas kernels, group_call(): pl.pallas_call(kernel, in_specs=[sspec, sspec, anyspec, vspec, vspec, any...  139 us
    dot_general x1, matrix products, fast_step(): u = jnp.dot(nt, w_loc, preferred_element_type=F32).astype(BF16)  19.1 us
    pallas_call x1, Pallas kernels, table_grad_call(): pl.pallas_call(kernel, grid_spec=pltpu.PrefetchScalarGridSpec(num_scalar_...  12 us
    unnamed x4, local copies, waits for them, and re-layouts  9.25 us
    pallas_call x1, Pallas kernels, pack_call(): pl.pallas_call(kernel, in_specs=[vspec, vspec], out_specs=[vspec] * 5, ou...  8.36 us
  transfers between devices with their start and end apart: 1, of which 1 were waited for; matrix products, arithmetic and copies ran while one was open for 10% of the time, Pallas kernels for 0%

profile of v2, /device:TPU:81, one launch (start us, length us, event | category | flops | bytes accessed | tf_op | source)
XLA Modules:
  0.0 198.9 jit_solution(16597058423201131237)
XLA Ops:
  0.6 0.8 copy.14
  1.4 0.1 copy.15
  1.5 0.7 reshape.172.ids_ref
  2.3 8.4 %pack_rows.1 = (s32[8,512]{1,0:T(8,128)S(1)}, s32[1,640]{1,0:T(1,128)S(1)}, s32[1,768]{1,0:T(1,128)S(1)}, s32[8,64]{1,0:T(8,128)S(1)}, bf16[640,1024]{1,0:T(8,128)(2,1)}) custom-call(s32[8,512]{1,0:T(8,128)} %reshape.172.ids_ref, bf16[2048,1024]{1,0:T(8,128)(2,1)} %e_ref.1), custom_call_target="tpu_custom_call" | custom-call | tf_op jit(solution)/shard_map/pack_rows/pallas_call | solution.py:145
  10.6 0.5 fusion.19
  12.5 178.0 %conditional.1 = (bf16[32,128,1408]{2,1,0:T(8,128)(2,1)}, bf16[32,16,1024]{2,1,0:T(8,128)(2,1)}, f32[2048,1024]{1,0:T(8,128)}, f32[1024,1408]{1,0:T(8,128)}, f32[1024]{0:T(1024)S(1)}) conditional(s32[]{:T(128)} %bitcast.8, (bf16[1024]{0:T(1024)(128)(2,1)}, s32[32,128]{1,0:T(8,128)}, bf16[32,16,1024]{2,1,0:T(8,128)(2,1)}, ...), branch_computations={%region_0.10_spmd, %region_10.11_spmd} | conditional | flops 13816927232 | bytes 53082264 | solution.py:553
  12.7 1.3 reshape.162.g_ref
  13.9 138.8 %group_rows.1 = (bf16[5120,1024]{1,0:T(8,128)(2,1)}, bf16[32,8,16,1024]{3,2,1,0:T(8,128)(2,1)}, bf16[32,16,1024]{2,1,0:T(8,128)(2,1)}, bf16[768,1024]{1,0:T(8,12...) custom-call(s32[8,512]{1,0:T(8,128)S(1)} %get-tuple-element.217.gidx_ref, s32[1,768]{1,0:T(1,128)S(1)} %get-tuple-element.218.inv_ref, ...), custom_call_target="tpu_custom_call" | custom-call | tf_op jit(solution)/shard_map/cond/branch_1_fun/group_rows/pallas_call | solution.py:445
  152.7 3.9 %all-to-all-start = ((bf16[8,96,1024]{2,1,0:T(8,128)(2,1)}), bf16[8,96,1024]{2,1,0:T(8,128)(2,1)S(1)}, u32[]{:S(2)}, u32[]{:S(2)}) async-start(bf16[8,96,1024]{2,1,0:T(8,128)(2,1)} %bitcast.69), calls=%async_computation | async-start | bytes 3145728 | tf_op jit(solution)/shard_map/cond/branch_1_fun/all_to_all | solution.py:537
  156.6 19.1 %convolution_convert_fusion = bf16[4096,1408]{1,0:T(8,128)(2,1)} fusion(bf16[4096,1024]{1,0:T(8,128)(2,1)} %bitcast.73, bf16[1024,1408]{1,0:T(8,128)(2,1)} %get-tuple-element.221.w_ref), kind=kOutput, calls=%fused_computation.2 | convolution fusion | flops 11816927232 | bytes 22806528 | tf_op jit(solution)/shard_map/cond/branch_1_fun/dot_general | solution.py:536
  175.7 1.6 all-to-all-done
  177.3 0.0 copy-start.1
  177.3 1.1 copy-done.1
  178.5 12.0 %table_grad.1 = f32[2048,1024]{1,0:T(8,128)} custom-call(s32[1,640]{1,0:T(1,128)S(1)} %get-tuple-element.226.id_ref, s32[8,64]{1,0:T(8,128)S(1)} %get-tuple-element.227.stat_ref, bf16[768,1024]{1,0:T(8,128)(2,1)} %bitcast.68), custom_call_target="tpu_custom_call" | custom-call | flops 2000000000 | bytes 12000000 | tf_op jit(solution)/shard_map/cond/branch_1_fun/table_grad/pallas_call | solution.py:514
  190.5 2.3 %copy.50 = bf16[32,16,1024]{2,1,0:T(8,128)(2,1)} copy(bf16[32,16,1024]{2,1,0:T(8,128)(2,1)} %get-tuple-element.501) | data formatting | bytes 2097152
  192.8 5.5 %copy.51 = f32[1024,1408]{1,0:T(8,128)} copy(f32[1024,1408]{1,0:T(8,128)} %get-tuple-element.503) | data formatting | bytes 11534336
  198.3 0.6 copy.52
Async XLA Ops:
  152.7 24.6 %all-to-all-start = ((bf16[8,96,1024]{2,1,0:T(8,128)(2,1)}), bf16[8,96,1024]{2,1,0:T(8,128)(2,1)S(1)}, u32[]{:S(2)}, u32[]{:S(2)}) async-start(bf16[8,96,1024]{2,1,0:T(8,128)(2,1)} %bitcast.69), calls=%async_computation | async-start | bytes 3145728 | tf_op jit(solution)/shard_map/cond/branch_1_fun/all_to_all | solution.py:537
  177.3 1.1 copy-start.1

commit v3 on v2

--- a/solution.py
+++ b/solution.py
@@ -75,7 +75,7 @@
     sub = 64
     ids_h = token_ids.reshape(n_micro, group_size, seq_loc).transpose(1, 0, 2).reshape(group_size, per)
 
-    def kernel(ids_ref, e_ref, gidx_ref, pid_ref, inv_ref, stat_ref, p_ref, rows, stage, pid_s, sem):
+    def kernel(ids_ref, e_ref, gidx_ref, pid_ref, inv_ref, stat_ref, tgt_ref, p_ref, rows, stage, pid_s, sem):
         me = lax.axis_index('tp')
         ids = ids_ref[...]
         owner = ids // rows_loc
@@ -120,6 +120,11 @@
             acc = acc + place(mine[h:h + 1], local[h:h + 1], cap)
         pid = (acc[0:1] * 64.0 + acc[1:2]).astype(jnp.int32)
         pid_ref[...] = pid
+        pair = jnp.where(owner == me, rk, -1)
+        for h in range(group_size):
+            got = place(pair[h:h + 1], local[h:h + 1] + 1, cap2)
+            row = (got[0:1] * 64.0 + got[1:2]).astype(jnp.int32)
+            tgt_ref[h:h + 1, :] = jnp.where(row == 0, rows_loc, row - 1)
         own = lax.broadcasted_iota(jnp.int32, (group_size, 1), 0) == me
         slot2 = jnp.sum(jnp.where(own, owner * cap2 + rk, 0), axis=0, keepdims=True)
         put = place(slot2, lax.broadcasted_iota(jnp.int32, (1, per), 1), slots)
@@ -145,11 +150,12 @@
     return pl.pallas_call(
         kernel,
         in_specs=[vspec, vspec],
-        out_specs=[vspec] * 5,
+        out_specs=[vspec] * 6,
         out_shape=[jax.ShapeDtypeStruct((group_size, per), jnp.int32),
                    jax.ShapeDtypeStruct((1, cap), jnp.int32),
                    jax.ShapeDtypeStruct((1, slots), jnp.int32),
                    jax.ShapeDtypeStruct((8, pairs), jnp.int32),
+                   jax.ShapeDtypeStruct((group_size, cap2), jnp.int32),
                    jax.ShapeDtypeStruct((cap, dim), BF16)],
         scratch_shapes=[pltpu.VMEM((rows_loc, 8, LANES), F32), pltpu.VMEM((cap, 8, LANES), F32),
                         pltpu.SMEM((1, cap), jnp.int32), pltpu.SemaphoreType.DMA(())],
@@ -194,8 +200,8 @@
     far = chips // 2
 
     def kernel(gidx_ref, inv_ref, p_ref, g_ref, w_ref, du_ref, r_ref,
-               pall_ref, n_ref, x_ref, pack_ref, dg_ref, dw_ref,
-               rows, land, stage, nbuf, ntr, dub, part, relay_in, relay_p, relay_out,
+               pall_ref, n_ref, x_ref, pack_ref, dg_ref, dw_out,
+               rows, land, stage, nbuf, ntr, dub, dw_ref, part, relay_in, relay_p, relay_out,
                own_p, direct, summed, dg_all, land_sem, du_sem, n_sem, send, recv):
         me = lax.axis_index('tp')
         c = me // 2
@@ -227,9 +233,14 @@
         def blk(d, off=0, n=cap):
             return pall_ref.at[pl.ds(pl.multiple_of(d * cap + off, 16), n), :]
 
-        go(rcopy(p_ref, blk(me), 0, 0, right))
-        go(rcopy(p_ref, blk(me), 1, 1, left))
+        def ph(i):
+            return p_ref.at[pl.ds(i * hcap, hcap), :]
+
+        go(rcopy(ph(0), blk(me, 0, hcap), 0, 0, right))
+        go(rcopy(ph(1), blk(me, hcap, hcap), 1, 1, left))
         go(rcopy(p_ref, blk(me), 2, 2, partner))
+        go(rcopy(ph(1), blk(me, hcap, hcap), 31, 31, right))
+        go(rcopy(ph(0), blk(me, 0, hcap), 32, 32, left))
 
         def du_copy(d, slot):
             return pltpu.make_async_copy(du_ref.at[:, d], dub.at[slot], du_sem.at[slot])
@@ -261,7 +272,15 @@
             go(rcopy(part.at[d, pl.ds(0, half)], relay_in.at[0, k], 9 + kk, 9 + k, dev(chips - 1, kk)))
             go(rcopy(part.at[d, pl.ds(half, half)], relay_in.at[1, k], 11 + kk, 11 + k, dev(1, kk)))
 
+        arrived(blk(left, 0, hcap), 0)
+        go(rcopy(blk(left, 0, hcap), blk(left, 0, hcap), 3, 3, right))
+        arrived(blk(right, hcap, hcap), 1)
+        go(rcopy(blk(right, hcap, hcap), blk(right, hcap, hcap), 4, 4, left))
         first_hop(0)
+        first_hop(1)
+        for kk in range(2):
+            go(rcopy(part.at[dev(chips - 1, kk), pl.ds(half, half)], direct.at[1, k], 13 + kk, 13 + k, dev(chips - 1, kk)))
+            go(rcopy(part.at[dev(1, kk), pl.ds(0, half)], direct.at[0, k], 15 + kk, 15 + k, dev(1, kk)))
         dl, dr = dev(chips - 1, 1 - k), dev(1, 1 - k)
         go(rcopy(part.at[dl, pl.ds(0, half)], relay_p.at[0], 17, 17, partner))
         go(rcopy(part.at[dr, pl.ds(half, half)], relay_p.at[1], 18, 18, partner))
@@ -282,16 +301,10 @@
         arrived(blk(partner), 2)
         convert(blk(partner), partner * cap, cap)
 
-        arrived(blk(left), 0)
-        go(rcopy(blk(left, 0, hcap), blk(left, 0, hcap), 3, 3, right))
-        arrived(blk(right), 1)
-        go(rcopy(blk(right, hcap, hcap), blk(right, hcap, hcap), 4, 4, left))
+        arrived(blk(left, hcap, hcap), 31)
         go(rcopy(blk(left), blk(left), 5, 5, partner))
+        arrived(blk(right, 0, hcap), 32)
         go(rcopy(blk(right), blk(right), 6, 6, partner))
-        first_hop(1)
-        for kk in range(2):
-            go(rcopy(part.at[dev(chips - 1, kk), pl.ds(half, half)], direct.at[1, k], 13 + kk, 13 + k, dev(chips - 1, kk)))
-            go(rcopy(part.at[dev(1, kk), pl.ds(0, half)], direct.at[0, k], 15 + kk, 15 + k, dev(1, kk)))
         convert(blk(left), left * cap, cap)
         convert(blk(right), right * cap, cap)
         pl_, pr_ = dev(chips - 1, 1 - k), dev(1, 1 - k)
@@ -302,12 +315,14 @@
         fk, fp = dev(far, k), dev(far, 1 - k)
         arrived(blk(fk, 0, hcap), 3)
         go(rcopy(blk(fk, 0, hcap), blk(fk, 0, hcap), 7, 7, partner))
+        convert(blk(fk, 0, hcap), fk * cap, hcap)
         arrived(blk(fk, hcap, hcap), 4)
         go(rcopy(blk(fk, hcap, hcap), blk(fk, hcap, hcap), 8, 8, partner))
-        convert(blk(fk), fk * cap, cap)
+        convert(blk(fk, hcap, hcap), fk * cap + hcap, hcap)
         arrived(blk(fp, 0, hcap), 7)
+        convert(blk(fp, 0, hcap), fp * cap, hcap)
         arrived(blk(fp, hcap, hcap), 8)
-        convert(blk(fp), fp * cap, cap)
+        convert(blk(fp, hcap, hcap), fp * cap + hcap, hcap)
 
         relays = [[rcopy(relay_out.at[s, pl.ds(q * piece, piece)], summed.at[s, pl.ds(q * piece, piece)],
                          20 + 2 * s + q, 20 + 2 * s + q, left if s == 0 else right) for q in range(2)] for s in range(2)]
@@ -340,7 +355,7 @@
         def chunk(h, carry):
             slot = h % 2
 
-            @pl.when(h == 2)
+            @pl.when(h == 3)
             def _():
                 relay()
 
@@ -383,6 +398,8 @@
                     dw_ref[:, t:t + w] += contrib
             return carry
         lax.fori_loop(0, group_size, chunk, 0)
+        dw_copy = pltpu.make_async_copy(dw_ref, dw_out, land_sem)
+        dw_copy.start()
         n_copy(group_size - 2, 0).wait()
         n_copy(group_size - 1, 1).wait()
 
@@ -433,6 +450,7 @@
         for o in range(1, group_size):
             dg = dg + dg_all[o]
         dg_ref[...] = dg
+        dw_copy.wait()
         for cp in sent:
             cp.wait_send()
         for s in range(2):
@@ -445,7 +463,7 @@
     return pl.pallas_call(
         kernel,
         in_specs=[sspec, sspec, anyspec, vspec, vspec, anyspec, vspec],
-        out_specs=[anyspec, anyspec, vspec, vspec, vspec, vspec],
+        out_specs=[anyspec, anyspec, vspec, vspec, vspec, anyspec],
         out_shape=[jax.ShapeDtypeStruct((group_size * cap, dim), BF16),
                    jax.ShapeDtypeStruct((n_micro, group_size, seq_loc, dim), BF16),
                    jax.ShapeDtypeStruct((n_micro, seq_loc, dim), BF16),
@@ -458,6 +476,7 @@
                         pltpu.VMEM((2, n_micro, seq_loc, dim), BF16),
                         pltpu.VMEM((dim, per), BF16),
                         pltpu.VMEM((2, n_micro, seq_loc, cols), BF16),
+                        pltpu.VMEM((dim, cols), F32),
                         pltpu.VMEM((group_size, per, dim), BF16),
                         pltpu.VMEM((2, 2, half, dim), BF16),
                         pltpu.VMEM((2, half, dim), BF16),
@@ -469,64 +488,91 @@
                         pltpu.SemaphoreType.DMA(()),
                         pltpu.SemaphoreType.DMA((2,)),
                         pltpu.SemaphoreType.DMA((2,)),
-                        pltpu.SemaphoreType.DMA((32,)),
-                        pltpu.SemaphoreType.DMA((32,))],
+                        pltpu.SemaphoreType.DMA((33,)),
+                        pltpu.SemaphoreType.DMA((33,))],
         compiler_params=pltpu.CompilerParams(collective_id=0, has_side_effects=True, vmem_limit_bytes=66_900_000),
         name="group_rows",
     )(gidx, inv2, p_own, gain.reshape(1, dim), w_loc, du4, dres)
 
 
-def table_grad_call(recv, packid, stat, rows_loc, cap2):
+def table_grad_call(recv, tgt, dw, x, rows_loc):
     slots, dim = recv.shape
-    group_size = slots // cap2
+    group_size, cap2 = tgt.shape
     sub = 64
     steps = 8
     blk = rows_loc // steps
-
-    def kernel(id_ref, stat_ref, r_ref, o_ref, rows, acc):
-        c = pl.program_id(0)
-        first = lax.axis_index('tp') * group_size
-
-        @pl.when(c == 0)
-        def _():
-            def zero(i, carry):
-                acc[pl.ds(i * sub, sub)] = jnp.zeros((sub, 8, LANES), F32)
+    unroll = 16
+
+    def kernel(tgt_ref, r_ref, dw_in, x_in, o_ref, dw_out, x_out, land, rows, acc, out, dw_v, x_v, sem_r, sem_o, sem_w, sem_x):
+        def local(a, b, s):
+            return pltpu.make_async_copy(a, b, s)
+
+        first = local(r_ref, land, sem_r)
+        first.start()
+        dw1, dw2 = local(dw_in, dw_v, sem_w), local(dw_v, dw_out, sem_w)
+        x1, x2 = local(x_in, x_v, sem_x), local(x_v, x_out, sem_x)
+        dw1.start()
+        x1.start()
+
+        def zero(i, carry):
+            acc[pl.ds(i * sub, sub)] = jnp.zeros((sub, 8, LANES), F32)
+            return carry
+        lax.fori_loop(0, rows_loc // sub, zero, 0)
+        first.wait()
+
+        def conv(i, carry):
+            off = pl.multiple_of(i * sub, sub)
+            to_rows(rows, off, land[pl.ds(off, sub), :].astype(F32))
+            return carry
+        lax.fori_loop(0, slots // sub, conv, 0)
+        dw1.wait()
+        dw2.start()
+        x1.wait()
+        x2.start()
+        for h in range(group_size):
+            def add(i, carry):
+                for j in range(unroll):
+                    r = i * unroll + j
+                    t = tgt_ref[h, r]
+                    acc[t] = acc[t] + rows[h * cap2 + r]
                 return carry
-            lax.fori_loop(0, rows_loc // sub, zero, 0)
-
-            def conv(i, carry):
+            lax.fori_loop(0, cap2 // unroll, add, 0)
+
+        def put(c):
+            return local(out.at[c % 2], o_ref.at[pl.ds(c * blk, blk), :], sem_o.at[c % 2])
+
+        for c in range(steps):
+            if c >= 2:
+                put(c - 2).wait()
+
+            def body(i, carry):
                 off = pl.multiple_of(i * sub, sub)
-                to_rows(rows, off, r_ref[pl.ds(off, sub), :].astype(F32))
+                out[c % 2, pl.ds(off, sub), :] = from_rows(acc, c * blk + off, sub)
                 return carry
-            lax.fori_loop(0, slots // sub, conv, 0)
-            for h in range(group_size):
-                b = stat_ref[1, first + h]
-
-                def add(r, carry):
-                    t = id_ref[0, b + r]
-                    acc[t] += rows[h * cap2 + r]
-                    return carry
-                lax.fori_loop(0, stat_ref[0, first + h], add, 0)
-
-        for i in range(blk // sub):
-            o_ref[i * sub:(i + 1) * sub, :] = from_rows(acc, c * blk + i * sub, sub)
-
+            lax.fori_loop(0, blk // sub, body, 0)
+            put(c).start()
+        put(steps - 2).wait()
+        put(steps - 1).wait()
+        dw2.wait()
+        x2.wait()
+
+    anyspec = pl.BlockSpec(memory_space=pl.ANY)
     return pl.pallas_call(
         kernel,
-        grid_spec=pltpu.PrefetchScalarGridSpec(
-            num_scalar_prefetch=2, grid=(steps,),
-            in_specs=[pl.BlockSpec((slots, dim), lambda c, *_: (0, 0))],
-            out_specs=pl.BlockSpec((blk, dim), lambda c, *_: (c, 0)),
-            scratch_shapes=[pltpu.VMEM((slots, 8, LANES), F32), pltpu.VMEM((rows_loc, 8, LANES), F32)]),
-        out_shape=jax.ShapeDtypeStruct((rows_loc, dim), F32),
-        compiler_params=pltpu.CompilerParams(dimension_semantics=("arbitrary",), vmem_limit_bytes=VMEM_MAX),
-        cost_estimate=pl.CostEstimate(flops=2_000_000_000, bytes_accessed=12_000_000, transcendentals=0),
+        in_specs=[pl.BlockSpec(memory_space=pltpu.SMEM), anyspec, anyspec, anyspec],
+        out_specs=[anyspec] * 3,
+        out_shape=[jax.ShapeDtypeStruct((rows_loc, dim), F32), jax.ShapeDtypeStruct(dw.shape, dw.dtype), jax.ShapeDtypeStruct(x.shape, x.dtype)],
+        scratch_shapes=[pltpu.VMEM((slots, dim), BF16), pltpu.VMEM((slots, 8, LANES), F32), pltpu.VMEM((rows_loc + 8, 8, LANES), F32),
+                        pltpu.VMEM((2, blk, dim), F32), pltpu.VMEM(dw.shape, dw.dtype), pltpu.VMEM(x.shape, x.dtype),
+                        pltpu.SemaphoreType.DMA(()), pltpu.SemaphoreType.DMA((2,)), pltpu.SemaphoreType.DMA(()), pltpu.SemaphoreType.DMA(())],
+        compiler_params=pltpu.CompilerParams(vmem_limit_bytes=VMEM_MAX),
+        cost_estimate=pl.CostEstimate(flops=2_000_000_000, bytes_accessed=24_000_000, transcendentals=0),
         name="table_grad",
-    )(packid, stat, recv)
+    )(tgt, recv, dw, x)
 
 
 def fast_step(tables, table_loc, gain_vec, w_loc, du_loc, dres_loc, group_size, cap, cap2):
-    gidx, packid, inv2, stat, mine = tables
+    gidx, _, inv2, _, tgt, mine = tables
     n_micro, seq_len, cols = du_loc.shape
     seq_loc = seq_len // group_size
     rows_loc, dim = table_loc.shape
@@ -535,7 +581,7 @@
     nt = normed.reshape(n_micro * seq_len, dim)
     u = jnp.dot(nt, w_loc, preferred_element_type=F32).astype(BF16)
     recv = lax.all_to_all(dx_pack.reshape(group_size, cap2, dim), 'tp', 0, 0, tiled=True)
-    grad_table = table_grad_call(recv.reshape(group_size * cap2, dim), packid, stat, rows_loc, cap2)
+    grad_table, grad_w, x_own = table_grad_call(recv.reshape(group_size * cap2, dim), tgt, grad_w, x_own, rows_loc)
     grad_gain = dg.reshape(dim)
     return u.reshape(n_micro, seq_len, cols), x_own, grad_table, grad_w, grad_gain
 
@@ -547,7 +593,7 @@
         rows_loc = table_loc.shape[0]
         tokens = token_ids.shape[0] * token_ids.shape[1]
         cap = tokens // group_size * 5 // 4
-        cap2 = tokens // group_size // group_size * 3 // 2
+        cap2 = tokens // group_size // group_size * 7 // 4
         tables = pack_call(token_ids, table_loc, group_size, cap, cap2)
         ok = (tables[3][2, 0] <= cap) & (tables[3][3, 0] <= cap2)
         return lax.cond(

time: 200 us -> 186 us (0.930)
  Pallas kernels: 159 us -> 149 us
  local copies, waits for them, and re-layouts: 13 us -> 6.04 us
  waiting for transfers between devices: 1.62 us -> 4.42 us
    pallas_call x1, Pallas kernels: 139 us -> 127 us  [group_call(): pl.pallas_call(kernel, in_specs=[sspec, sspec, anyspec, vspec, vspec, any...]
    unnamed x4 -> x2, local copies, waits for them, and re-layouts: 9.25 us -> 1.41 us
    all_to_all x1, waiting for transfers between devices: 1.62 us -> 4.42 us  [fast_step(): lax.all_to_all(dx_pack.reshape(group_size, cap2, dim), 'tp', 0, 0, tiled=...]
where the time goes in v3:
time: 186 us; the launch traced here: 185 us
  Pallas kernels  149 us (80%)
  matrix products  19.1 us (10%)
  local copies, waits for them, and re-layouts  6.04 us (3%)
  waiting for transfers between devices  4.42 us (2%)
  starting transfers between devices  3.92 us (2%)
  between operations  1.96 us (1%)
    pallas_call x1, Pallas kernels, group_call(): pl.pallas_call(kernel, in_specs=[sspec, sspec, anyspec, vspec, vspec, any...  127 us
    dot_general x1, matrix products, fast_step(): u = jnp.dot(nt, w_loc, preferred_element_type=F32).astype(BF16)  19.1 us
    pallas_call x1, Pallas kernels, table_grad_call(): pl.pallas_call(kernel, in_specs=[pl.BlockSpec(memory_space=pltpu.SMEM), a...  13.5 us
    pallas_call x1, Pallas kernels, pack_call(): pl.pallas_call(kernel, in_specs=[vspec, vspec], out_specs=[vspec] * 6, ou...  8.67 us
    all_to_all x1, waiting for transfers between devices, fast_step(): lax.all_to_all(dx_pack.reshape(group_size, cap2, dim), 'tp', 0, 0, tiled=...  4.42 us
    all_to_all x1, starting transfers between devices, fast_step(): lax.all_to_all(dx_pack.reshape(group_size, cap2, dim), 'tp', 0, 0, tiled=...  3.92 us
  transfers between devices with their start and end apart: 1, of which 1 were waited for; matrix products, arithmetic and copies ran while one was open for 10% of the time, Pallas kernels for 0%

profile of v3, /device:TPU:81, one launch (start us, length us, event | category | flops | bytes accessed | tf_op | source)
XLA Modules:
  0.0 184.8 jit_solution(5876547263575115733)
XLA Ops:
  0.6 0.8 copy.14
  1.4 0.1 copy.15
  1.5 0.7 reshape.172.ids_ref
  2.3 8.7 %pack_rows.1 = (s32[8,512]{1,0:T(8,128)S(1)}, s32[1,640]{1,0:T(1,128)}, s32[1,896]{1,0:T(1,128)S(1)}, s32[8,64]{1,0:T(8,128)}, s32[8,112]{1,0:T(8,128)S(1)}, /*index=5*/bf16[640,1024]{1,0:T(8,128)(2,1)}) custom-call(s32[8,512]{1,0:T(8,128)} %reshape.172.ids_ref, bf16[2048,1024]{1,0:T(8,128)(2,1)} %e_ref.1), custom_call_target="tpu_custom_call" | custom-call | tf_op jit(solution)/shard_map/pack_rows/pallas_call | solution.py:150
  10.9 1.3 fusion.19
  13.5 170.7 %conditional.1 = (bf16[32,128,1408]{2,1,0:T(8,128)(2,1)}, bf16[32,16,1024]{2,1,0:T(8,128)(2,1)}, f32[2048,1024]{1,0:T(8,128)}, f32[1024,1408]{1,0:T(8,128)}, f32[1024]{0:T(1024)S(1)}) conditional(s32[]{:T(128)} %bitcast.8, (bf16[1024]{0:T(1024)(128)(2,1)}, s32[32,128]{1,0:T(8,128)}, bf16[32,16,1024]{2,1,0:T(8,128)(2,1)}, ...), branch_computations={%region_0.10_spmd, %region_10.11_spmd} | conditional | flops 13816927232 | bytes 59655780 | solution.py:599
  13.7 1.3 reshape.162.g_ref
  15.0 126.8 %group_rows.1 = (bf16[5120,1024]{1,0:T(8,128)(2,1)}, bf16[32,8,16,1024]{3,2,1,0:T(8,128)(2,1)}, bf16[32,16,1024]{2,1,0:T(8,128)(2,1)}, bf16[896,1024]{1,0:T(8,12...) custom-call(s32[8,512]{1,0:T(8,128)S(1)} %get-tuple-element.215.gidx_ref, s32[1,896]{1,0:T(1,128)S(1)} %get-tuple-element.216.inv_ref, ...), custom_call_target="tpu_custom_call" | custom-call | tf_op jit(solution)/shard_map/cond/branch_1_fun/group_rows/pallas_call | solution.py:463
  141.8 3.9 %all-to-all-start = ((bf16[8,112,1024]{2,1,0:T(8,128)(2,1)}), bf16[8,112,1024]{2,1,0:T(8,128)(2,1)S(1)}, u32[]{:S(2)}, u32[]{:S(2)}) async-start(bf16[8,112,1024]{2,1,0:T(8,128)(2,1)} %bitcast.69), calls=%async_computation | async-start | bytes 3670016 | tf_op jit(solution)/shard_map/cond/branch_1_fun/all_to_all | solution.py:583
  145.7 19.1 %convolution_convert_fusion = bf16[4096,1408]{1,0:T(8,128)(2,1)} fusion(bf16[4096,1024]{1,0:T(8,128)(2,1)} %bitcast.73, bf16[1024,1408]{1,0:T(8,128)(2,1)} %get-tuple-element.219.w_ref), kind=kOutput, calls=%fused_computation.2 | convolution fusion | flops 11816927232 | bytes 22806528 | tf_op jit(solution)/shard_map/cond/branch_1_fun/dot_general | solution.py:582
  164.8 4.4 %all-to-all-done = bf16[8,112,1024]{2,1,0:T(8,128)(2,1)S(1)} async-done(((bf16[8,112,1024]{2,1,0:T(8,128)(2,1)}), bf16[8,112,1024]{2,1,0:T(8,128)(2,1)S(1)}, u32[]{:S(2)}, u32[]{:S(2)}) %all-to-all-start) | async-done | bytes 1835040 | tf_op jit(solution)/shard_map/cond/branch_1_fun/all_to_all | solution.py:583
  169.2 0.0 copy-start.1
  169.2 1.3 copy-done.1
  170.5 13.5 %table_grad.1 = (f32[2048,1024]{1,0:T(8,128)}, f32[1024,1408]{1,0:T(8,128)}, bf16[32,16,1024]{2,1,0:T(8,128)(2,1)}) custom-call(s32[8,112]{1,0:T(8,128)S(1)} %get-tuple-element.223.tgt_ref, bf16[896,1024]{1,0:T(8,128)(2,1)} %bitcast.68, f32[1024,1408]{1,0:T(8,128)} %get-tuple-element.225.dw_in, bf16[32,16,1024]{2,1,0:T(8,128)(2,1)} %get-tuple-element.226.x_in), custom_call_target="tpu_custom_call" | custom-call | flops 2000000000 | bytes 24000000 | tf_op jit(solution)/shard_map/cond/branch_1_fun/table_grad/pallas_call | solution.py:560
  184.2 0.6 copy.48
Async XLA Ops:
  141.8 27.4 %all-to-all-start = ((bf16[8,112,1024]{2,1,0:T(8,128)(2,1)}), bf16[8,112,1024]{2,1,0:T(8,128)(2,1)S(1)}, u32[]{:S(2)}, u32[]{:S(2)}) async-start(bf16[8,112,1024]{2,1,0:T(8,128)(2,1)} %bitcast.69), calls=%async_computation | async-start | bytes 3670016 | tf_op jit(solution)/shard_map/cond/branch_1_fun/all_to_all | solution.py:583
  169.2 1.3 copy-start.1

commit v4 on v3

--- a/solution.py
+++ b/solution.py
@@ -347,7 +347,7 @@
                 for s in range(2):
                     relays[s][q].start()
 
-        gf = g_ref[...].astype(F32)
+        gf = g_ref[...].astype(F32).reshape(1, dim)
 
         def n_copy(h, slot):
             return pltpu.make_async_copy(nbuf.at[slot], n_ref.at[:, h], n_sem.at[slot])
@@ -492,7 +492,7 @@
                         pltpu.SemaphoreType.DMA((33,))],
         compiler_params=pltpu.CompilerParams(collective_id=0, has_side_effects=True, vmem_limit_bytes=66_900_000),
         name="group_rows",
-    )(gidx, inv2, p_own, gain.reshape(1, dim), w_loc, du4, dres)
+    )(gidx, inv2, p_own, gain, w_loc, du4, dres)
 
 
 def table_grad_call(recv, tgt, dw, x, rows_loc):
@@ -571,19 +571,14 @@
     )(tgt, recv, dw, x)
 
 
-def fast_step(tables, table_loc, gain_vec, w_loc, du_loc, dres_loc, group_size, cap, cap2):
-    gidx, _, inv2, _, tgt, mine = tables
-    n_micro, seq_len, cols = du_loc.shape
-    seq_loc = seq_len // group_size
-    rows_loc, dim = table_loc.shape
-    du4 = du_loc.reshape(n_micro, group_size, seq_loc, cols)
-    _, normed, x_own, dx_pack, dg, grad_w = group_call(mine, gidx, inv2, gain_vec, w_loc, du4, dres_loc, cap, cap2)
-    nt = normed.reshape(n_micro * seq_len, dim)
-    u = jnp.dot(nt, w_loc, preferred_element_type=F32).astype(BF16)
+def exchange(normed, x_own, dx_pack, dg, grad_w, tgt, w_loc, rows_loc):
+    n_micro, group_size, seq_loc, dim = normed.shape
+    cap2 = tgt.shape[1]
+    cols = w_loc.shape[1]
+    u = jnp.dot(normed.reshape(-1, dim), w_loc, preferred_element_type=F32).astype(BF16)
     recv = lax.all_to_all(dx_pack.reshape(group_size, cap2, dim), 'tp', 0, 0, tiled=True)
     grad_table, grad_w, x_own = table_grad_call(recv.reshape(group_size * cap2, dim), tgt, grad_w, x_own, rows_loc)
-    grad_gain = dg.reshape(dim)
-    return u.reshape(n_micro, seq_len, cols), x_own, grad_table, grad_w, grad_gain
+    return u.reshape(n_micro, group_size * seq_loc, cols), x_own, grad_table, grad_w, dg.reshape(dim)
 
 
 def solution(mesh):
@@ -594,13 +589,16 @@
         tokens = token_ids.shape[0] * token_ids.shape[1]
         cap = tokens // group_size * 5 // 4
         cap2 = tokens // group_size // group_size * 7 // 4
-        tables = pack_call(token_ids, table_loc, group_size, cap, cap2)
-        ok = (tables[3][2, 0] <= cap) & (tables[3][3, 0] <= cap2)
+        n_micro, seq_len, cols = du_loc.shape
+        gidx, _, inv2, stat, tgt, mine = pack_call(token_ids, table_loc, group_size, cap, cap2)
+        ok = (stat[2, 0] <= cap) & (stat[3, 0] <= cap2)
+        du4 = du_loc.reshape(n_micro, group_size, seq_len // group_size, cols)
+        _, *mid = group_call(mine, gidx, inv2, gain_vec, w_loc, du4, dres_loc, cap, cap2)
         return lax.cond(
             ok,
-            lambda t, i, *a: fast_step(t, *a, group_size, cap, cap2),
-            lambda t, i, *a: slow_step(i, *a, group_size),
-            tuple(tables), token_ids, table_loc, gain_vec, w_loc, du_loc, dres_loc)
+            lambda mid, tgt, i, t, g, w, *a: exchange(*mid, tgt, w, rows_loc),
+            lambda mid, tgt, *a: slow_step(*a, group_size),
+            tuple(mid), tgt, token_ids, table_loc, gain_vec, w_loc, du_loc, dres_loc)
 
     return jax.shard_map(local_step, mesh=mesh,
                          in_specs=(P('dp', None), P('tp', None), P(None), P(None, 'tp'), P('dp', None, 'tp'), P('dp', 'tp', None)),

time: 186 us -> 184 us (0.989)
  no operation moved by 1% of the time
where the time goes in v4:
time: 184 us; the launch traced here: 183 us
  Pallas kernels  149 us (81%)
  matrix products  19.1 us (10%)
  local copies, waits for them, and re-layouts  4.85 us (3%)
  waiting for transfers between devices  4.35 us (2%)
  starting transfers between devices  3.92 us (2%)
  between operations  2.03 us (1%)
    pallas_call x1, Pallas kernels, group_call(): pl.pallas_call(kernel, in_specs=[sspec, sspec, anyspec, vspec, vspec, any...  127 us
    dot_general x1, matrix products, exchange(): jnp.dot(normed.reshape(-1, dim), w_loc, preferred_element_type=F32)  19.1 us
    pallas_call x1, Pallas kernels, table_grad_call(): pl.pallas_call(kernel, in_specs=[pl.BlockSpec(memory_space=pltpu.SMEM), a...  13.3 us
    pallas_call x1, Pallas kernels, pack_call(): pl.pallas_call(kernel, in_specs=[vspec, vspec], out_specs=[vspec] * 6, ou...  8.66 us
    all_to_all x1, waiting for transfers between devices, exchange(): lax.all_to_all(dx_pack.reshape(group_size, cap2, dim), 'tp', 0, 0, tiled=...  4.35 us
    all_to_all x1, starting transfers between devices, exchange(): lax.all_to_all(dx_pack.reshape(group_size, cap2, dim), 'tp', 0, 0, tiled=...  3.92 us
  transfers between devices with their start and end apart: 1, of which 1 were waited for; matrix products, arithmetic and copies ran while one was open for 10% of the time, Pallas kernels for 0%

profile of v4, /device:TPU:81, one launch (start us, length us, event | category | flops | bytes accessed | tf_op | source)
XLA Modules:
  0.0 183.3 jit_solution(15835494068683836423)
XLA Ops:
  0.6 0.8 copy.14
  1.4 0.1 copy.15
  1.5 0.7 reshape.169.ids_ref
  2.3 8.7 %pack_rows.1 = (s32[8,512]{1,0:T(8,128)}, s32[1,640]{1,0:T(1,128)}, s32[1,896]{1,0:T(1,128)}, s32[8,64]{1,0:T(8,128)}, s32[8,112]{1,0:T(8,128)S(1)}, /*index=5*/bf16[640,1024]{1,0:T(8,128)(2,1)}) custom-call(s32[8,512]{1,0:T(8,128)} %reshape.169.ids_ref, bf16[2048,1024]{1,0:T(8,128)(2,1)} %e_ref.1), custom_call_target="tpu_custom_call" | custom-call | tf_op jit(solution)/shard_map/pack_rows/pallas_call | solution.py:150
  10.9 1.4 fusion.19
  13.6 0.0 copy-start.3
  13.7 126.8 %group_rows.1 = (bf16[5120,1024]{1,0:T(8,128)(2,1)}, bf16[32,8,16,1024]{3,2,1,0:T(8,128)(2,1)}, bf16[32,16,1024]{2,1,0:T(8,128)(2,1)}, bf16[896,1024]{1,0:T(8,12...) custom-call(s32[8,512]{1,0:T(8,128)} %get-tuple-element.239.gidx_ref, s32[1,896]{1,0:T(1,128)} %get-tuple-element.240.inv_ref, ...), custom_call_target="tpu_custom_call" | custom-call | tf_op jit(solution)/shard_map/group_rows/pallas_call | solution.py:463
  140.5 0.0 copy-done.3
  140.5 42.2 %conditional.1 = (bf16[32,128,1408]{2,1,0:T(8,128)(2,1)}, bf16[32,16,1024]{2,1,0:T(8,128)(2,1)}, f32[2048,1024]{1,0:T(8,128)}, f32[1024,1408]{1,0:T(8,128)}, f32[1024]{0:T(1024)S(1)}) conditional(s32[]{:T(128)} %bitcast.7, (bf16[1024]{0:T(1024)(128)(2,1)S(1)}, s32[32,128]{1,0:T(8,128)}, bf16[32,16,1024]{2,1,0:T(8,128)(2,1)}, ...), branch_computations={%region_0.10_spmd, %region_10.11_spmd} | conditional | flops 13816927232 | bytes 63846016 | solution.py:597
  140.7 3.9 %all-to-all-start = ((bf16[8,112,1024]{2,1,0:T(8,128)(2,1)}), bf16[8,112,1024]{2,1,0:T(8,128)(2,1)S(1)}, u32[]{:S(2)}, u32[]{:S(2)}) async-start(bf16[8,112,1024]{2,1,0:T(8,128)(2,1)} %bitcast.69), calls=%async_computation | async-start | bytes 3670016 | tf_op jit(solution)/shard_map/cond/branch_1_fun/all_to_all | solution.py:579
  144.7 0.0 copy-start.2
  144.7 19.1 %convolution_convert_fusion = bf16[4096,1408]{1,0:T(8,128)(2,1)} fusion(bf16[4096,1024]{1,0:T(8,128)(2,1)} %bitcast.73, bf16[1024,1408]{1,0:T(8,128)(2,1)} %get-tuple-element.214), kind=kOutput, calls=%fused_computation.2 | convolution fusion | flops 11816927232 | bytes 22806528 | tf_op jit(solution)/shard_map/cond/branch_1_fun/dot_general | solution.py:578
  163.8 4.4 %all-to-all-done = bf16[8,112,1024]{2,1,0:T(8,128)(2,1)S(1)} async-done(((bf16[8,112,1024]{2,1,0:T(8,128)(2,1)}), bf16[8,112,1024]{2,1,0:T(8,128)(2,1)S(1)}, u32[]{:S(2)}, u32[]{:S(2)}) %all-to-all-start) | async-done | bytes 1835040 | tf_op jit(solution)/shard_map/cond/branch_1_fun/all_to_all | solution.py:579
  168.1 0.0 copy-start.1
  168.1 1.3 copy-done.1
  169.4 0.0 copy-done.2
  169.4 13.3 %table_grad.1 = (f32[2048,1024]{1,0:T(8,128)}, f32[1024,1408]{1,0:T(8,128)}, bf16[32,16,1024]{2,1,0:T(8,128)(2,1)}) custom-call(s32[8,112]{1,0:T(8,128)S(1)} %get-tuple-element.215.tgt_ref, bf16[896,1024]{1,0:T(8,128)(2,1)} %bitcast.68, f32[1024,1408]{1,0:T(8,128)} %get-tuple-element.217.dw_in, bf16[32,16,1024]{2,1,0:T(8,128)(2,1)S(1)} %copy-done.2), custom_call_target="tpu_custom_call" | custom-call | flops 2000000000 | bytes 24000000 | tf_op jit(solution)/shard_map/cond/branch_1_fun/table_grad/pallas_call | solution.py:560
  182.7 0.6 copy.48
Async XLA Ops:
  13.6 126.9 %copy-start.3 = (bf16[1024]{0:T(1024)(128)(2,1)S(1)}, bf16[1024]{0:T(1024)(128)(2,1)}, u32[]{:S(2)}) copy-start(bf16[1024]{0:T(1024)(128)(2,1)} %g_ref.1) | copy-start | bytes 6148
  140.7 27.4 %all-to-all-start = ((bf16[8,112,1024]{2,1,0:T(8,128)(2,1)}), bf16[8,112,1024]{2,1,0:T(8,128)(2,1)S(1)}, u32[]{:S(2)}, u32[]{:S(2)}) async-start(bf16[8,112,1024]{2,1,0:T(8,128)(2,1)} %bitcast.69), calls=%async_computation | async-start | bytes 3670016 | tf_op jit(solution)/shard_map/cond/branch_1_fun/all_to_all | solution.py:579
  144.7 24.7 %copy-start.2 = (bf16[32,16,1024]{2,1,0:T(8,128)(2,1)S(1)}, bf16[32,16,1024]{2,1,0:T(8,128)(2,1)}, u32[]{:S(2)}) copy-start(bf16[32,16,1024]{2,1,0:T(8,128)(2,1)} %get-tuple-element.218.x_in) | copy-start | bytes 3145732 | tf_op jit(solution)/shard_map/cond
  168.1 1.3 copy-start.1
